TPU v7x, 8 devices: a whole 2x2x1 slice. The times are simulated.
8 devices in a mesh: fsdp: 8 (over z, y, x, core).
Axes of the slice: x: 2, y: 2, z: 1, core: 2. Of those that a mesh axis runs over, the one named last changes fastest.
Arguments:
- tokens: int32 [64, 256], P('fsdp')
- positions: int32 [64, 256], P('fsdp')
- embed_table: bfloat16 [152064, 1024], P('fsdp')
- attn_norm: bfloat16 [1024], P('fsdp')
- w_query: bfloat16 [1024, 2048], P('fsdp')
- w_key: bfloat16 [1024, 1024], P('fsdp')
- w_value: bfloat16 [1024, 1024], P('fsdp')
- q_norm: bfloat16 [128], replicated
- k_norm: bfloat16 [128], replicated
- w_out: bfloat16 [2048, 1024], P('fsdp')
- mlp_norm: bfloat16 [1024], P('fsdp')
- w_gate: bfloat16 [1024, 3072], P('fsdp')
- w_up: bfloat16 [1024, 3072], P('fsdp')
- w_down: bfloat16 [3072, 1024], P('fsdp')
- dy_out: bfloat16 [64, 256, 1024], P('fsdp')
Outputs:
- output 1: bfloat16 [64, 256, 1024], P('fsdp')
- output 2: float32 [152064, 1024], P('fsdp')
- output 3: float32 [1024], P('fsdp')
- output 4: float32 [1024, 2048], P('fsdp')
- output 5: float32 [1024, 1024], P('fsdp')
- output 6: float32 [1024, 1024], P('fsdp')
- output 7: float32 [128], replicated
- output 8: float32 [128], replicated
- output 9: float32 [2048, 1024], P('fsdp')
- output 10: float32 [1024], P('fsdp')
- output 11: float32 [1024, 3072], P('fsdp')
- output 12: float32 [1024, 3072], P('fsdp')
- output 13: float32 [3072, 1024], P('fsdp')
All inputs are finite; a program needn't handle non-finite values.
Results may differ from a plain program's by a relative error of at most 0.0159861.
Values are sent between devices in bfloat16 or wider.
A program may use at most 1 GiB of HBM per device.

v0:
```python
import math
import jax
import jax.numpy as jnp
from jax import lax
from jax.sharding import PartitionSpec as P

NORM_EPS = 1e-6
ROPE_THETA = 1.0e6
AXIS_NAME = 'fsdp'
SHARDED = (True, True, True, True, False, False, True, True, True, True, True)


def rope_tables(positions, head_dim):
    half_dim = head_dim // 2
    inv_freq = jnp.exp(jnp.arange(half_dim, dtype=jnp.float32) * (-2.0 * math.log(ROPE_THETA) / head_dim))
    angles = positions.astype(jnp.float32)[:, :, None] * inv_freq
    return jnp.cos(angles), jnp.sin(angles)


def rotate(values, cos_t, sin_t):
    half_dim = values.shape[-1] // 2
    lead_half = values[..., :half_dim]
    tail_half = values[..., half_dim:]
    return jnp.concatenate([lead_half * cos_t - tail_half * sin_t, tail_half * cos_t + lead_half * sin_t], axis=-1)


def norm_fwd(values):
    values_f = values.astype(jnp.float32)
    inv_rms = lax.rsqrt(jnp.mean(values_f * values_f, axis=-1, keepdims=True) + NORM_EPS)
    return values_f * inv_rms, inv_rms


def norm_bwd(grad_out, normed, inv_rms, norm_gain):
    grad_normed = grad_out * norm_gain.astype(jnp.float32)
    mean_term = jnp.mean(grad_normed * normed, axis=-1, keepdims=True)
    return inv_rms * (grad_normed - normed * mean_term)


def attn_fwd(q_rot, k_rot, v_raw):
    seq_len = q_rot.shape[1]
    attn_scale = q_rot.shape[-1] ** -0.5
    scores = jnp.einsum('bqgrh,bkgh->bgrqk', q_rot, k_rot, preferred_element_type=jnp.float32) * attn_scale
    causal = lax.broadcasted_iota(jnp.int32, (seq_len, seq_len), 0) >= lax.broadcasted_iota(jnp.int32, (seq_len, seq_len), 1)
    attn_probs = jax.nn.softmax(jnp.where(causal, scores, -1e30), axis=-1)
    attn_heads = jnp.einsum('bgrqk,bkgh->bqgrh', attn_probs.astype(jnp.bfloat16), v_raw, preferred_element_type=jnp.float32)
    return attn_heads.astype(jnp.bfloat16), attn_probs


def attn_bwd(grad_out, q_rot, k_rot, v_raw, attn_probs):
    attn_scale = q_rot.shape[-1] ** -0.5
    grad_b = grad_out.astype(jnp.bfloat16)
    probs_b = attn_probs.astype(jnp.bfloat16)
    grad_probs = jnp.einsum('bqgrh,bkgh->bgrqk', grad_b, v_raw, preferred_element_type=jnp.float32)
    grad_v = jnp.einsum('bgrqk,bqgrh->bkgh', probs_b, grad_b, preferred_element_type=jnp.float32)
    grad_scores = attn_probs * (grad_probs - jnp.sum(grad_probs * attn_probs, axis=-1, keepdims=True)) * attn_scale
    scores_b = grad_scores.astype(jnp.bfloat16)
    grad_q = jnp.einsum('bgrqk,bkgh->bqgrh', scores_b, k_rot, preferred_element_type=jnp.float32)
    grad_k = jnp.einsum('bgrqk,bqgrh->bkgh', scores_b, q_rot, preferred_element_type=jnp.float32)
    return grad_q, grad_k, grad_v


def layer_fwd(x_emb, positions, weights):
    attn_norm, w_query, w_key, w_value, q_norm, k_norm, w_out, mlp_norm, w_gate, w_up, w_down = weights
    batch_len, seq_len, model_dim = x_emb.shape
    head_dim = q_norm.shape[0]
    kv_heads = w_key.shape[1] // head_dim
    q_per_kv = w_query.shape[1] // w_key.shape[1]
    cos_t, sin_t = rope_tables(positions, head_dim)
    cos_q = cos_t[:, :, None, None, :]
    sin_q = sin_t[:, :, None, None, :]
    cos_k = cos_t[:, :, None, :]
    sin_k = sin_t[:, :, None, :]
    normed1, norm1_inv = norm_fwd(x_emb)
    attn_in = (normed1 * attn_norm.astype(jnp.float32)).astype(jnp.bfloat16)
    q_raw = jnp.einsum('bsd,dn->bsn', attn_in, w_query, preferred_element_type=jnp.float32).astype(jnp.bfloat16).reshape(batch_len, seq_len, kv_heads, q_per_kv, head_dim)
    k_raw = jnp.einsum('bsd,dn->bsn', attn_in, w_key, preferred_element_type=jnp.float32).astype(jnp.bfloat16).reshape(batch_len, seq_len, kv_heads, head_dim)
    v_raw = jnp.einsum('bsd,dn->bsn', attn_in, w_value, preferred_element_type=jnp.float32).astype(jnp.bfloat16).reshape(batch_len, seq_len, kv_heads, head_dim)
    q_normed, q_inv = norm_fwd(q_raw)
    k_normed, k_inv = norm_fwd(k_raw)
    q_rot = rotate(q_normed * q_norm.astype(jnp.float32), cos_q, sin_q).astype(jnp.bfloat16)
    k_rot = rotate(k_normed * k_norm.astype(jnp.float32), cos_k, sin_k).astype(jnp.bfloat16)
    attn_heads, attn_probs = attn_fwd(q_rot, k_rot, v_raw)
    attn_flat = attn_heads.reshape(batch_len, seq_len, -1)
    attn_proj = jnp.einsum('bsn,nd->bsd', attn_flat, w_out, preferred_element_type=jnp.float32)
    hidden = (x_emb.astype(jnp.float32) + attn_proj).astype(jnp.bfloat16)
    normed2, norm2_inv = norm_fwd(hidden)
    mlp_in = (normed2 * mlp_norm.astype(jnp.float32)).astype(jnp.bfloat16)
    gate_pre = jnp.einsum('bsd,df->bsf', mlp_in, w_gate, preferred_element_type=jnp.float32)
    up_proj = jnp.einsum('bsd,df->bsf', mlp_in, w_up, preferred_element_type=jnp.float32)
    mlp_act = (jax.nn.silu(gate_pre) * up_proj).astype(jnp.bfloat16)
    mlp_proj = jnp.einsum('bsf,fd->bsd', mlp_act, w_down, preferred_element_type=jnp.float32)
    layer_out = (hidden.astype(jnp.float32) + mlp_proj).astype(jnp.bfloat16)
    saved_acts = (normed1, norm1_inv, attn_in, q_normed, q_inv, k_normed, k_inv, q_rot, k_rot, v_raw, attn_probs, attn_flat, normed2, norm2_inv, mlp_in, gate_pre, up_proj, mlp_act, cos_q, sin_q, cos_k, sin_k)
    return layer_out, saved_acts


def layer_bwd(dy_out, saved_acts, weights):
    attn_norm, w_query, w_key, w_value, q_norm, k_norm, w_out, mlp_norm, w_gate, w_up, w_down = weights
    (normed1, norm1_inv, attn_in, q_normed, q_inv, k_normed, k_inv, q_rot, k_rot, v_raw, attn_probs, attn_flat, normed2, norm2_inv, mlp_in, gate_pre, up_proj, mlp_act, cos_q, sin_q, cos_k, sin_k) = saved_acts
    batch_len, seq_len, model_dim = dy_out.shape
    grad_w_down = jnp.einsum('bsf,bsd->fd', mlp_act, dy_out, preferred_element_type=jnp.float32)
    grad_act = jnp.einsum('bsd,fd->bsf', dy_out, w_down, preferred_element_type=jnp.float32)
    gate_sig = jax.nn.sigmoid(gate_pre)
    grad_gate = (grad_act * up_proj * gate_sig * (1.0 + gate_pre * (1.0 - gate_sig))).astype(jnp.bfloat16)
    grad_up = (grad_act * gate_pre * gate_sig).astype(jnp.bfloat16)
    grad_w_gate = jnp.einsum('bsd,bsf->df', mlp_in, grad_gate, preferred_element_type=jnp.float32)
    grad_w_up = jnp.einsum('bsd,bsf->df', mlp_in, grad_up, preferred_element_type=jnp.float32)
    grad_mlp_in = jnp.einsum('bsf,df->bsd', grad_gate, w_gate, preferred_element_type=jnp.float32) + jnp.einsum('bsf,df->bsd', grad_up, w_up, preferred_element_type=jnp.float32)
    grad_mlp_norm = jnp.sum(grad_mlp_in * normed2, axis=(0, 1))
    grad_hidden = dy_out.astype(jnp.float32) + norm_bwd(grad_mlp_in, normed2, norm2_inv, mlp_norm)
    hidden_b = grad_hidden.astype(jnp.bfloat16)
    grad_w_out = jnp.einsum('bsn,bsd->nd', attn_flat, hidden_b, preferred_element_type=jnp.float32)
    grad_heads = jnp.einsum('bsd,nd->bsn', hidden_b, w_out, preferred_element_type=jnp.float32).reshape(q_rot.shape)
    grad_q, grad_k, grad_v = attn_bwd(grad_heads, q_rot, k_rot, v_raw, attn_probs)
    grad_qt = rotate(grad_q, cos_q, -sin_q)
    grad_kt = rotate(grad_k, cos_k, -sin_k)
    grad_q_norm = jnp.sum(grad_qt * q_normed, axis=(0, 1, 2, 3))
    grad_k_norm = jnp.sum(grad_kt * k_normed, axis=(0, 1, 2))
    grad_q_raw = norm_bwd(grad_qt, q_normed, q_inv, q_norm).astype(jnp.bfloat16).reshape(batch_len, seq_len, -1)
    grad_k_raw = norm_bwd(grad_kt, k_normed, k_inv, k_norm).astype(jnp.bfloat16).reshape(batch_len, seq_len, -1)
    grad_v_raw = grad_v.astype(jnp.bfloat16).reshape(batch_len, seq_len, -1)
    grad_w_query = jnp.einsum('bsd,bsn->dn', attn_in, grad_q_raw, preferred_element_type=jnp.float32)
    grad_w_key = jnp.einsum('bsd,bsn->dn', attn_in, grad_k_raw, preferred_element_type=jnp.float32)
    grad_w_value = jnp.einsum('bsd,bsn->dn', attn_in, grad_v_raw, preferred_element_type=jnp.float32)
    grad_attn_in = (jnp.einsum('bsn,dn->bsd', grad_q_raw, w_query, preferred_element_type=jnp.float32)
                    + jnp.einsum('bsn,dn->bsd', grad_k_raw, w_key, preferred_element_type=jnp.float32)
                    + jnp.einsum('bsn,dn->bsd', grad_v_raw, w_value, preferred_element_type=jnp.float32))
    grad_attn_norm = jnp.sum(grad_attn_in * normed1, axis=(0, 1))
    grad_x_emb = grad_hidden + norm_bwd(grad_attn_in, normed1, norm1_inv, attn_norm)
    return grad_x_emb, (grad_attn_norm, grad_w_query, grad_w_key, grad_w_value, grad_q_norm, grad_k_norm, grad_w_out, grad_mlp_norm, grad_w_gate, grad_w_up, grad_w_down)


def solution(mesh):
    row_spec = P(AXIS_NAME, None)
    vec_spec = P(AXIS_NAME)
    full_spec = P(None)
    batch_spec = P(AXIS_NAME, None, None)
    weight_specs = (vec_spec, row_spec, row_spec, row_spec, full_spec, full_spec, row_spec, vec_spec, row_spec, row_spec, row_spec)

    def device_step(tokens, positions, table_shard, attn_norm, w_query, w_key, w_value, q_norm, k_norm, w_out, mlp_norm, w_gate, w_up, w_down, dy_out):
        shards = (attn_norm, w_query, w_key, w_value, q_norm, k_norm, w_out, mlp_norm, w_gate, w_up, w_down)
        weights = tuple(lax.all_gather(w_shard, AXIS_NAME, tiled=True) if is_sharded else w_shard for w_shard, is_sharded in zip(shards, SHARDED))
        batch_len, seq_len = tokens.shape
        rows_local, model_dim = table_shard.shape
        all_ids = lax.all_gather(tokens.reshape(-1), AXIS_NAME, tiled=True)
        local_ids = all_ids - lax.axis_index(AXIS_NAME) * rows_local
        is_owner = (local_ids >= 0) & (local_ids < rows_local)
        picked = jnp.take(table_shard, jnp.clip(local_ids, 0, rows_local - 1), axis=0)
        picked = jnp.where(is_owner[:, None], picked, jnp.zeros((), picked.dtype))
        x_emb = lax.psum_scatter(picked, AXIS_NAME, scatter_dimension=0, tiled=True).reshape(batch_len, seq_len, model_dim)
        layer_out, saved_acts = layer_fwd(x_emb, positions, weights)
        grad_x_emb, grad_full = layer_bwd(dy_out, saved_acts, weights)
        grad_shards = tuple(lax.psum_scatter(grad_part, AXIS_NAME, scatter_dimension=0, tiled=True) if is_sharded else lax.psum(grad_part, AXIS_NAME) for grad_part, is_sharded in zip(grad_full, SHARDED))
        all_rows = lax.all_gather(grad_x_emb.reshape(-1, model_dim), AXIS_NAME, tiled=True)
        d_table = jax.ops.segment_sum(all_rows, jnp.where(is_owner, local_ids, rows_local), num_segments=rows_local)
        return (layer_out, d_table) + grad_shards

    return jax.shard_map(device_step, mesh=mesh, in_specs=(row_spec, row_spec, row_spec) + weight_specs + (batch_spec,), out_specs=(batch_spec, row_spec) + weight_specs, check_vma=False)
```

profile of v0, /device:TPU:0, one launch (start us, length us, event | category | flops | bytes accessed | tf_op | source)
XLA Modules:
  0.0 2673.6 jit_solution(17909502279973144620)
XLA Ops:
  8.7 14.2 all_gather.33
  23.6 453.9 %gather_fusion = bf16[16384,1024]{1,0:T(8,128)(2,1)} fusion(bf16[19008,1024]{1,0:T(8,128)(2,1)} %param.17, s32[16384]{0:T(1024)S(1)} %get-tuple-element.43), kind=kCustom, calls=%fused_computation | custom fusion | bytes 67174400 | tf_op jit(solution)/shard_map/jit(_take)/gather | solution.py:148
  477.5 22.7 select_select_fusion
  504.4 377.3 %all-gather = bf16[8,1,128]{2,1,0:T(2,128)(2,1)S(1)} all-gather(bf16[1,1,128]{2,1,0:T(2,128)(2,1)S(1)} %bitcast.254), channel_id=1, replica_groups=mesh['fsdp'=8] {'fsdp'}, dimensions={0}, use_global_device_ids=true | all-gather | bytes 2304 | tf_op jit(solution)/shard_map/all_gather | solution.py:142
  881.8 10.7 all-gather.1
  899.0 20.8 fusion.45
  919.8 143.5 %reduce-scatter.9.cloned.1.call-done = bf16[2048,1024]{1,0:T(8,128)(2,1)} async-done(((bf16[16384,1024]{1,0:T(8,128)(2,1)}), bf16[2048,1024]{1,0:T(8,128)(2,1)}) %reduce-scatter.9.cloned.1.call-update) | async-done | bytes 4194320 | tf_op jit(solution)/shard_map/reduce_scatter | solution.py:150
  1066.4 20.7 all-gather.13.cloned.1.call-done
  1087.1 7.5 convolution_convert_fusion.1
  1100.7 6.9 fusion.41
  1107.6 11.9 all-gather.15.cloned.1.call-done
  1119.6 15.3 convert_convert_fusion
  1134.9 22.1 reshape.166
  1156.9 23.7 multiply_reduce_fusion.2
  1186.0 10.7 fusion.15
  1196.7 8.7 subtract_convert_fusion
  1205.4 9.6 convolution_convert_fusion.2
  1215.0 10.6 subtract_convert_fusion.1
  1232.5 26.3 fusion.98
  1258.8 17.6 fusion.42
  1276.4 15.2 fusion.30
  1291.7 20.1 fusion.51
  1311.8 39.9 %multiply_convert_fusion.1 = (bf16[8,256,3072]{2,1,0:T(8,128)(2,1)}, bf16[8,256,3072]{2,1,0:T(8,128)(2,1)}, bf16[8,256,3072]{2,1,0:T(8,128)(2,1)}) fusion(f32[8,256,3072]{2,1,0:T(8,128)} %fusion.45, f32[8,256,3072]{2,1,0:T(8,128)} %fusion.51, bf16[1024,3072]{1,0:T(8,128)(2,1)} %all-gather.19.cloned.1.call-done, ...), kind=kOutput, calls=%fused_computation.18 | convolution fusion | flops 12993953792 | bytes 98578432 | tf_op jit(solution)/shard_map/bsd,df->bsf/dot_general | solution.py:88
  1351.7 18.9 fusion.49
  1370.6 23.4 fusion.29
  1394.0 7.2 fusion.28
  1404.5 11.2 convolution_convert_fusion
  1415.6 11.8 copy.281
  1427.5 20.3 fusion.64
  1447.7 50.3 %fusion.69 = f32[8,256,8,128]{3,1,2,0:T(8,128)} fusion(f32[8,8,256,256,2]{3,2,4,1,0:T(8,128)} %fusion.64, bf16[8,256,8,2,64]{4,1,3,2,0:T(8,128)(2,1)} %get-tuple-element.35, bf16[8,256,8,2,64]{4,1,3,2,0:T(8,128)(2,1)} %get-tuple-element.34, f32[8,8,2,256,256]{3,4,2,1,0:T(8,128)} %get-tuple-element.50, f32[8,8,2,256]{3,2,1,0:T(2,128)S(1)} %copy-done.47), kind=kOutput, calls=%fused_computation.119 | convolution fusion | flops 2223014144 | bytes 84017152 | tf_op jit(solution)/shard_map/bgrqk,bqgrh->bkgh/dot_general | solution.py:58
  1498.0 51.8 %fusion.23 = f32[8,256,8,2,128]{4,1,3,2,0:T(8,128)} fusion(f32[8,8,256,256,2]{3,2,4,1,0:T(8,128)} %fusion.64, bf16[8,256,8,64]{3,1,2,0:T(8,128)(2,1)} %get-tuple-element.41, bf16[8,256,8,64]{3,1,2,0:T(8,128)(2,1)} %get-tuple-element.40, f32[8,8,2,256,256]{3,4,2,1,0:T(8,128)} %get-tuple-element.50, f32[8,8,2,256]{3,2,1,0:T(2,128)S(1)} %copy-done.47), kind=kOutput, calls=%fused_computation.46 | convolution fusion | flops 2214625536 | bytes 88211456 | tf_op jit(solution)/shard_map/bgrqk,bkgh->bqgrh/dot_general | solution.py:57
  1554.5 16.8 bitcast_convert_fusion
  1571.4 10.3 multiply_subtract_fusion.1
  1581.6 9.6 fusion.70
  1596.2 9.4 mul.512
  1610.1 9.2 mul.498
  1619.3 19.5 multiply_subtract_fusion
  1638.8 20.2 multiply_reduce_fusion.1
  1663.7 21.7 mul.494
  1685.5 21.6 mul.495
  1707.0 28.7 %copy.229 = f32[8,256,8,2,128]{4,3,2,1,0:T(2,128)} copy(f32[8,256,8,2,128]{4,1,3,2,0:T(8,128)} %get-tuple-element.24) | data formatting | bytes 33554432 | tf_op jit(solution)/shard_map/concatenate | solution.py:24
  1735.7 21.6 concatenate.21
  1757.3 21.8 mul.448.clone
  1779.0 21.8 mul.478
  1800.8 11.5 fusion.36
  1812.4 28.4 %multiply_reduce_fusion = (f32[2048]{0:T(1024)}, bf16[8,256,2048]{2,1,0:T(8,128)(2,1)}) fusion(f32[8,256,2048]{2,1,0:T(8,128)} %concatenate.21, f32[8,256,2048]{2,1,0:T(8,128)} %convert_convert_fusion, f32[8,256,2048]{2,1,0:T(8,128)} %mul.478, f32[8,256,2048]{2,1,0:T(8,128)} %mul.495, f32[2048]{0:T(1024)S(1)} %bitcast.245), kind=kLoop, calls=%fused_computation.23 | loop fusion | flops 33552384 | bytes 75513856 | tf_op jit(solution)/shard_map/reduce_sum | solution.py:117
  1840.8 6.9 fusion.79
  1847.7 12.9 fusion.60
  1860.6 13.8 multiply_reduce_fusion.3
  1874.5 9.6 multiply_add_fusion.1
  1884.2 10.2 convolution_bitcast_fusion.6
  1897.9 6.1 convolution_bitcast_fusion.5
  1904.3 15.1 convolution_bitcast_fusion.4
  1919.5 15.8 convolution_bitcast_fusion.3
  1936.0 19.9 convolution_bitcast_fusion.2
  1956.0 19.9 convolution_bitcast_fusion.1
  1976.2 19.3 convolution_bitcast_fusion
  1996.4 7.1 sort
  2003.6 23.6 all-reduce.2
  2028.3 19.8 fusion.31
  2048.2 134.7 %all-gather.25.cloned.1.call-done = f32[16384,1024]{1,0:T(8,128)} async-done(((f32[2048,1024]{1,0:T(8,128)}), f32[16384,1024]{1,0:T(8,128)}) %all-gather.25.cloned.1.call-update) | async-done | bytes 67108880 | tf_op jit(solution)/shard_map/all_gather | solution.py:154
  2182.9 306.9 %scatter_custom_fusion = f32[19008,1024]{1,0:T(8,128)} fusion(s32[16384]{0:T(1024)S(1)} %get-tuple-element.13, f32[16384,1024]{1,0:T(8,128)} %all-gather.25.cloned.1.call-done, s32[16384]{0:T(1024)S(1)} %broadcast_clamp_fusion, f32[]{:T(128)} %constant.22.clone.1), kind=kCustom, calls=%fused_computation.5 | custom fusion | flops 16777216 | bytes 77857280 | tf_op jit(solution)/shard_map/scatter-add | solution.py:155
  2494.2 86.4 %reduce-scatter.21.cloned.1.call-done = f32[128,3072]{1,0:T(8,128)} async-done(((f32[1024,3072]{1,0:T(8,128)}), f32[128,3072]{1,0:T(8,128)}) %reduce-scatter.21.cloned.1.call-update) | async-done | bytes 1572880 | tf_op jit(solution)/shard_map/reduce_scatter | solution.py:153
  2580.5 86.4 %reduce-scatter.23.cloned.1.call-done = f32[384,1024]{1,0:T(8,128)} async-done(((f32[3072,1024]{1,0:T(8,128)}), f32[384,1024]{1,0:T(8,128)}) %reduce-scatter.23.cloned.1.call-update) | async-done | bytes 1572880 | tf_op jit(solution)/shard_map/reduce_scatter | solution.py:153
  (181 shorter events, 67.6 us)
Async XLA Ops:
  7.2 891.9 %all-gather.23.cloned.1.call-start = ((), (), s32[]{:S(2)}) async-start(), calls=%async_computation.15 | async-start | bytes 7077888 | tf_op jit(solution)/shard_map/all_gather | solution.py:142
  7.9 1055.4 %reduce-scatter.9.cloned.1.call-start = ((), (), s32[]{:S(2)}) async-start(), calls=%async_computation.8 | async-start | bytes 37748736 | tf_op jit(solution)/shard_map/reduce_scatter | solution.py:150
  500.2 4.1 copy-start.39
  500.2 381.5 %copy-start.45 = (bf16[128]{0:T(256)(128)(2,1)S(1)}, bf16[128]{0:T(256)(128)(2,1)}, u32[]{:S(2)}) copy-start(bf16[128]{0:T(256)(128)(2,1)} %param.23) | copy-start | bytes 772
  500.2 381.5 %copy-start.33 = (s32[8,256]{1,0:T(8,128)S(1)}, s32[8,256]{1,0:T(8,128)}, u32[]{:S(2)}) copy-start(s32[8,256]{1,0:T(8,128)} %param.16) | copy-start | bytes 24580
  500.2 381.5 %copy-start.41 = (bf16[128]{0:T(256)(128)(2,1)S(1)}, bf16[128]{0:T(256)(128)(2,1)}, u32[]{:S(2)}) copy-start(bf16[128]{0:T(256)(128)(2,1)} %param.22) | copy-start | bytes 772
  500.2 381.5 %copy-start.40 = (bf16[128]{0:T(256)(128)(2,1)S(1)}, bf16[128]{0:T(256)(128)(2,1)}, u32[]{:S(2)}) copy-start(bf16[128]{0:T(256)(128)(2,1)} %param.25) | copy-start | bytes 772
  500.3 586.8 %all-gather.13.cloned.1.call-start = ((), (), s32[]{:S(2)}) async-start(), calls=%async_computation.10 | async-start | bytes 2359296 | tf_op jit(solution)/shard_map/all_gather | solution.py:142
  501.0 618.5 %all-gather.15.cloned.1.call-start = ((), (), s32[]{:S(2)}) async-start(), calls=%async_computation.11 | async-start | bytes 4718592 | tf_op jit(solution)/shard_map/all_gather | solution.py:142
  501.6 703.8 %all-gather.11.cloned.1.call-start = ((), (), s32[]{:S(2)}) async-start(), calls=%async_computation.9 | async-start | bytes 2359296 | tf_op jit(solution)/shard_map/all_gather | solution.py:142
  502.2 774.2 %all-gather.17.cloned.1.call-start = ((), (), s32[]{:S(2)}) async-start(), calls=%async_computation.12 | async-start | bytes 4718592 | tf_op jit(solution)/shard_map/all_gather | solution.py:142
  502.8 788.9 %all-gather.21.cloned.1.call-start = ((), (), s32[]{:S(2)}) async-start(), calls=%async_computation.14 | async-start | bytes 7077888 | tf_op jit(solution)/shard_map/all_gather | solution.py:142
  503.5 808.3 %all-gather.19.cloned.1.call-start = ((), (), s32[]{:S(2)}) async-start(), calls=%async_computation.13 | async-start | bytes 7077888 | tf_op jit(solution)/shard_map/all_gather | solution.py:142
  504.3 1678.6 %all-gather.25.cloned.1.call-start = ((), (), s32[]{:S(2)}) async-start(), calls=%async_computation.16 | async-start | bytes 75497472 | tf_op jit(solution)/shard_map/all_gather | solution.py:154
  881.7 323.7 %copy-start.24 = (f32[8,1,128]{2,1,0:T(1,128)}, f32[8,1,128]{2,1,0:T(1,128)S(1)}, u32[]{:S(2)}) copy-start(f32[8,1,128]{2,1,0:T(1,128)S(1)} %convert_element_type.172) | copy-start | bytes 12292
  881.7 219.0 %copy-start.34 = (f32[128]{0:T(128)}, f32[128]{0:T(128)S(1)}, u32[]{:S(2)}) copy-start(f32[128]{0:T(128)S(1)} %convert_element_type.139) | copy-start | bytes 1540
  881.8 304.2 %copy-start.37 = (f32[128]{0:T(128)}, f32[128]{0:T(128)S(1)}, u32[]{:S(2)}) copy-start(f32[128]{0:T(128)S(1)} %convert_element_type.144) | copy-start | bytes 1540
  899.0 316.0 %copy-start.4 = (f32[8,256,64]{2,1,0:T(8,128)}, f32[8,256,64]{2,1,0:T(8,128)S(1)}, u32[]{:S(2)}) copy-start(f32[8,256,64]{2,1,0:T(8,128)S(1)} %get-tuple-element.48) | copy-start | bytes 1572868
  1066.4 28.3 %copy-start.22 = (f32[2048]{0:T(1024)}, f32[2048]{0:T(1024)S(1)}, u32[]{:S(2)}) copy-start(f32[2048]{0:T(1024)S(1)} %add_rsqrt_fusion.3) | copy-start | bytes 24580
  1066.4 139.0 %copy-start.20 = (f32[8,256]{1,0:T(8,128)}, f32[8,256]{1,0:T(8,128)S(1)}, u32[]{:S(2)}) copy-start(f32[8,256]{1,0:T(8,128)S(1)} %rsqrt.37) | copy-start | bytes 24580
  1094.6 2.0 copy-start.1
  1100.7 124.9 %copy-start.17 = (f32[8,256,8]{1,2,0:T(8,128)}, f32[8,256,8]{1,2,0:T(8,128)S(1)}, u32[]{:S(2)}) copy-start(f32[8,256,8]{1,2,0:T(8,128)S(1)} %add_rsqrt_fusion.1) | copy-start | bytes 196612
  1185.9 10.8 copy-start.15
  1186.0 10.7 copy-start.13
  1258.8 17.6 copy-start.46
  1276.4 15.3 copy-start.29
  1291.7 102.4 %copy-start.26 = (f32[8,256]{1,0:T(8,128)}, f32[8,256]{1,0:T(8,128)S(1)}, u32[]{:S(2)}) copy-start(f32[8,256]{1,0:T(8,128)S(1)} %add_rsqrt_fusion.2) | copy-start | bytes 24580
  1394.0 10.4 copy-start.43
  1401.3 3.2 copy-start.3
  1427.4 20.3 copy-start.47
  1498.0 51.8 %copy-start.16 = (f32[8,256,8,2]{1,2,3,0:T(8,128)S(1)}, f32[8,256,8,2]{1,2,3,0:T(8,128)}, u32[]{:S(2)}) copy-start(f32[8,256,8,2]{1,2,3,0:T(8,128)} %copy-done.15) | copy-start | bytes 393220
  1554.5 16.8 copy-start.5
  1554.5 16.8 copy-start.6
  1571.3 10.3 copy-start.2
  1571.3 10.3 copy-start.18
  1571.3 10.3 copy-start.35
  1596.2 9.4 copy-start.11
  1619.3 19.5 copy-start.14
  1619.3 19.5 copy-start.38
  1779.0 21.8 copy-start.31
  1800.8 11.5 copy-start.42
  1812.3 28.4 %copy-start.10 = (bf16[8,256,1024]{2,1,0:T(8,128)(2,1)}, bf16[8,256,1024]{2,1,0:T(8,128)(2,1)S(1)}, u32[]{:S(2)}) copy-start(bf16[8,256,1024]{2,1,0:T(8,128)(2,1)S(1)} %get-tuple-element.31) | copy-start | bytes 12582916
  1812.3 28.4 %copy-start.44 = (bf16[1024,1024]{1,0:T(8,128)(2,1)S(1)}, bf16[1024,1024]{1,0:T(8,128)(2,1)}, u32[]{:S(2)}) copy-start(bf16[1024,1024]{1,0:T(8,128)(2,1)} %all-gather.13.cloned.1.call-done) | copy-start | bytes 6291460
  1840.8 6.9 copy-start.7
  1847.6 13.0 copy-start
  1847.6 13.0 copy-start.8
  1847.7 13.0 copy-start.12
  1847.7 13.0 copy-start.21
  1847.7 13.0 copy-start.25
  1884.1 10.3 copy-start.23
  1884.1 605.7 %reduce-scatter.13.cloned.1.call-start = ((), (), s32[]{:S(2)}) async-start(), calls=%async_computation.18 | async-start | bytes 4718592 | tf_op jit(solution)/shard_map/reduce_scatter | solution.py:153
  1894.4 595.4 %reduce-scatter.15.cloned.1.call-start = ((), (), s32[]{:S(2)}) async-start(), calls=%async_computation.19 | async-start | bytes 4718592 | tf_op jit(solution)/shard_map/reduce_scatter | solution.py:153
  1894.5 3.5 copy-start.9
  1904.1 585.7 %reduce-scatter.11.cloned.1.call-start = ((), (), s32[]{:S(2)}) async-start(), calls=%async_computation.17 | async-start | bytes 9437184 | tf_op jit(solution)/shard_map/reduce_scatter | solution.py:153
  1919.5 570.4 %reduce-scatter.17.cloned.1.call-start = ((), (), s32[]{:S(2)}) async-start(), calls=%async_computation.20 | async-start | bytes 9437184 | tf_op jit(solution)/shard_map/reduce_scatter | solution.py:153
  1935.3 0.7 copy-start.27
  1935.3 0.7 copy-start.30
  1935.3 558.9 %reduce-scatter.19.cloned.1.call-start = ((), (), s32[]{:S(2)}) async-start(), calls=%async_computation.21 | async-start | bytes 14155776 | tf_op jit(solution)/shard_map/reduce_scatter | solution.py:153
  1955.9 624.6 %reduce-scatter.21.cloned.1.call-start = ((), (), s32[]{:S(2)}) async-start(), calls=%async_computation.22 | async-start | bytes 14155776 | tf_op jit(solution)/shard_map/reduce_scatter | solution.py:153
  1975.9 691.0 %reduce-scatter.23.cloned.1.call-start = ((), (), s32[]{:S(2)}) async-start(), calls=%async_computation.23 | async-start | bytes 14155776 | tf_op jit(solution)/shard_map/reduce_scatter | solution.py:153
  1995.5 0.8 copy-start.19
  1995.5 8.0 copy-start.28
  1995.5 8.1 copy-start.32
  1995.5 8.1 copy-start.36
Sparse Core Ops, SparseCore 0:
  9.8 42.5 all-gather.22
  500.4 562.8 reduce-scatter.8
  1065.1 21.9 all-gather.12
  1088.8 30.7 all-gather.14
  1121.2 21.9 all-gather.10
  1144.9 30.7 all-gather.16
  1177.5 39.5 all-gather.20
  1218.9 39.5 all-gather.18
  1884.2 298.5 all-gather.24
  2186.6 42.4 reduce-scatter.12
  2232.9 42.4 reduce-scatter.14
  2279.2 62.2 reduce-scatter.10
  2345.5 62.2 reduce-scatter.16
  2411.6 82.4 reduce-scatter.18
  2498.0 82.4 reduce-scatter.20
  2584.4 82.4 reduce-scatter.22
where the time goes:
time: 2690 us; the launch traced here: 2670 us
  local copies, waits for them, and re-layouts  686 us (26%)
  other arithmetic  529 us (20%)
  matrix products  525 us (20%)
  waiting for transfers between devices  492 us (18%)
  blocking collectives  426 us (16%)
    gather x1, local copies, waits for them, and re-layouts, device_step(): jnp.take(table_shard, jnp.clip(local_ids, 0, rows_local - 1), axis=0)  454 us
    all_gather x2, blocking collectives, device_step(): lax.all_gather(w_shard, AXIS_NAME, tiled=True)  388 us
    scatter-add x3, other arithmetic, device_step(): jax.ops.segment_sum(all_rows, jnp.where(is_owner, local_ids, rows_local),...  314 us
    reduce_scatter x7, waiting for transfers between devices, device_step(): lax.psum_scatter(grad_part, AXIS_NAME, scatter_dimension=0, tiled=True)  177 us
    reduce_scatter x1, waiting for transfers between devices, device_step(): lax.psum_scatter(picked, AXIS_NAME, scatter_dimension=0, tiled=True)  143 us
    all_gather x1, waiting for transfers between devices, device_step(): lax.all_gather(grad_x_emb.reshape(-1, model_dim), AXIS_NAME, tiled=True)  135 us
    mul x4, local copies, waits for them, and re-layouts, norm_fwd(): return (values_f * inv_rms, inv_rms)  57.3 us
    mul x4, local copies, waits for them, and re-layouts, norm_bwd(): return inv_rms * (grad_normed - normed * mean_term)  57.2 us
  transfers between devices with their start and end apart: 16, of which 7 were waited for; matrix products, arithmetic and copies ran while one was open for 44% of the time, Pallas kernels for 0%

commit v1 on v0

v1 whole, which is shorter than its diff:
```python
import functools
import math
import jax
import jax.numpy as jnp
from jax import lax
from jax.experimental import pallas as pl
from jax.experimental.pallas import tpu as pltpu
from jax.sharding import PartitionSpec as P

NORM_EPS = 1e-6
ROPE_THETA = 1.0e6
AXIS_NAME = 'fsdp'
F32 = jnp.float32
BF16 = jnp.bfloat16
LANES = 128
SUBL = 8
VMEM_LIMIT = 60 * 1024 * 1024


def dot_nt(a, b):
    return lax.dot_general(a, b, (((1,), (1,)), ((), ())), preferred_element_type=F32)


def dot_tn(a, b):
    return lax.dot_general(a, b, (((0,), (0,)), ((), ())), preferred_element_type=F32)


def dot_nn(a, b):
    return jnp.dot(a, b, preferred_element_type=F32)


def block_of(total, limit, step):
    best = step
    for size in range(step, limit + 1, step):
        if total % size == 0:
            best = size
    return best


def gather_body(n_tab, n_lead, tab_rows, tok_rows, idx_ref, tab_ref, lead_ref, tail_ref, store, stage):
    step = pl.program_id(0)

    @pl.when(step == 0)
    def _():
        store[n_tab * tab_rows] = jnp.zeros((SUBL, LANES), BF16)

    @pl.when(step < n_tab)
    def _():
        for lane in range(SUBL):
            stage[pl.ds(lane, tab_rows, stride=SUBL), :] = tab_ref[:, lane * LANES:(lane + 1) * LANES].astype(F32)
        rows = stage[...].reshape(tab_rows, SUBL, LANES)
        store[pl.ds(step * tab_rows, tab_rows)] = rows.astype(BF16)

    def copy_rows(out_ref):
        base = (step - n_tab) * tok_rows
        unroll = 16

        def loop(it, carry):
            first = it * unroll
            for u in range(unroll):
                out_ref[first + u] = store[idx_ref[base + first + u]]
            return carry

        lax.fori_loop(0, tok_rows // unroll, loop, 0)

    @pl.when((step >= n_tab) & (step < n_tab + n_lead))
    def _():
        copy_rows(lead_ref)

    @pl.when(step >= n_tab + n_lead)
    def _():
        copy_rows(tail_ref)


def table_gather(table, idx, lead):
    rows, width = table.shape
    total = idx.shape[0]
    tab_rows = block_of(rows, 640, 16)
    n_tab = rows // tab_rows
    tok_rows = 512
    n_lead, n_tail = lead // tok_rows, (total - lead) // tok_rows
    out_block = (tok_rows, SUBL, LANES)
    grid_spec = pltpu.PrefetchScalarGridSpec(
        num_scalar_prefetch=1,
        grid=(n_tab + n_lead + n_tail,),
        in_specs=[pl.BlockSpec((tab_rows, width), lambda s, ids: (jnp.minimum(s, n_tab - 1), 0))],
        out_specs=[pl.BlockSpec(out_block, lambda s, ids: (jnp.clip(s - n_tab, 0, n_lead - 1), 0, 0)),
                   pl.BlockSpec(out_block, lambda s, ids: (jnp.clip(s - n_tab - n_lead, 0, n_tail - 1), 0, 0))],
        scratch_shapes=[pltpu.VMEM((rows + 8, SUBL, LANES), BF16), pltpu.VMEM((tab_rows * SUBL, LANES), F32)],
    )
    return pl.pallas_call(
        functools.partial(gather_body, n_tab, n_lead, tab_rows, tok_rows),
        grid_spec=grid_spec,
        out_shape=[jax.ShapeDtypeStruct((n * tok_rows, SUBL, LANES), BF16) for n in (n_lead, n_tail)],
        compiler_params=pltpu.CompilerParams(dimension_semantics=("arbitrary",), vmem_limit_bytes=VMEM_LIMIT),
        cost_estimate=pl.CostEstimate(flops=70_000_000_000, bytes_accessed=rows * width * 2 + total * width * 2, transcendentals=0),
        name="table_gather",
    )(idx, table)


def scatter_body(group, slots, out_rows, perm_ref, sid_ref, bst_ref, rows_ref, out_ref, acc, ring, sem):
    blk = pl.program_id(0)
    total = bst_ref[pl.num_programs(0)]
    n_groups = (total + group - 1) // group

    def issue(g):
        slot = lax.rem(g, slots)
        for u in range(group):
            pltpu.make_async_copy(rows_ref.at[perm_ref[g * group + u]], ring.at[slot * group + u], sem.at[slot]).start()

    @pl.when(blk == 0)
    def _():
        def first(g, carry):
            issue(g)
            return carry

        lax.fori_loop(0, jnp.minimum(n_groups, slots), first, 0)

    acc[...] = jnp.zeros(acc.shape, F32)
    low = bst_ref[blk]
    high = bst_ref[blk + 1]
    g_first = low // group
    g_last = jnp.where(high > low, (high + group - 1) // group, g_first)
    base = blk * out_rows

    def per_group(g, carry):
        start = g * group
        slot = lax.rem(g, slots)

        @pl.when(start >= low)
        def _():
            pltpu.make_async_copy(rows_ref.at[pl.ds(0, group)], ring.at[pl.ds(slot * group, group)], sem.at[slot]).wait()

        prev, prev_id = carry
        for u in range(group):
            row_id = sid_ref[start + u]
            local = row_id - base
            inside = (local >= 0) & (local < out_rows)
            value = ring[slot * group + u]
            value = jnp.where(row_id == prev_id, prev + value, value)
            acc[pl.ds(pl.multiple_of(jnp.where(inside, local, out_rows) * SUBL, SUBL), SUBL), :] = value
            prev, prev_id = value, row_id

        @pl.when((high >= start + group) & (g + slots < n_groups))
        def _():
            issue(g + slots)

        return prev, prev_id

    lax.fori_loop(g_first, g_last, per_group, (jnp.zeros((SUBL, LANES), F32), jnp.int32(-1)))
    for lane in range(SUBL):
        out_ref[:, lane * LANES:(lane + 1) * LANES] = acc[pl.ds(lane, out_rows, stride=SUBL), :]


def table_scatter(rows, perm, sid, bst, n_rows, out_rows):
    total = rows.shape[0]
    width = SUBL * LANES
    group, slots = 16, 16
    grid_spec = pltpu.PrefetchScalarGridSpec(
        num_scalar_prefetch=3,
        grid=(n_rows // out_rows,),
        in_specs=[pl.BlockSpec(memory_space=pl.ANY)],
        out_specs=pl.BlockSpec((out_rows, width), lambda b, *_: (b, 0)),
        scratch_shapes=[pltpu.VMEM((out_rows * SUBL + SUBL, LANES), F32), pltpu.VMEM((group * slots, SUBL, LANES), F32), pltpu.SemaphoreType.DMA((slots,))],
    )
    return pl.pallas_call(
        functools.partial(scatter_body, group, slots, out_rows),
        grid_spec=grid_spec,
        out_shape=jax.ShapeDtypeStruct((n_rows, width), F32),
        compiler_params=pltpu.CompilerParams(dimension_semantics=("arbitrary",), vmem_limit_bytes=32 * 1024 * 1024),
        cost_estimate=pl.CostEstimate(flops=70_000_000_000, bytes_accessed=n_rows * width * 4 + total * width * 4, transcendentals=0),
        name="table_scatter",
    )(perm, sid, bst, rows)


def head_prep(raw, gain, cos_t, sin_t):
    values = raw.astype(F32)
    inv = lax.rsqrt(jnp.mean(values * values, axis=-1, keepdims=True) + NORM_EPS)
    normed = values * inv
    scaled = normed * gain
    rot = scaled * cos_t + pltpu.roll(scaled, LANES // 2, 1) * sin_t
    return rot.astype(BF16), normed, inv


def head_prep_bwd(grad, normed, inv, gain, cos_t, sin_t):
    grad_t = grad * cos_t - pltpu.roll(grad, LANES // 2, 1) * sin_t
    grad_gain = jnp.sum(grad_t * normed, axis=0, keepdims=True)
    grad_n = grad_t * gain
    mean_term = jnp.mean(grad_n * normed, axis=-1, keepdims=True)
    return (inv * (grad_n - normed * mean_term)).astype(BF16), grad_gain


def exp_scaled(scores, peak):
    return jnp.exp2((scores - peak) * (LANES ** -0.5 * math.log2(math.e)))


def probs_by_key(q_rot, k_rot, tri):
    h = tri.shape[0]
    top = dot_nt(k_rot[:h], q_rot)
    s_ll = jnp.where(tri, top[:, :h], -1e30)
    s_lh = top[:, h:]
    s_hh = jnp.where(tri, dot_nt(k_rot[h:], q_rot[h:]), -1e30)
    peak_l = jnp.max(s_ll, axis=0, keepdims=True)
    peak_h = jnp.maximum(jnp.max(s_lh, axis=0, keepdims=True), jnp.max(s_hh, axis=0, keepdims=True))
    e_ll, e_lh, e_hh = exp_scaled(s_ll, peak_l), exp_scaled(s_lh, peak_h), exp_scaled(s_hh, peak_h)
    r_l = 1.0 / jnp.sum(e_ll, axis=0, keepdims=True)
    r_h = 1.0 / (jnp.sum(e_lh, axis=0, keepdims=True) + jnp.sum(e_hh, axis=0, keepdims=True))
    return e_ll * r_l, e_lh * r_h, e_hh * r_h


def causal_by_key(seq):
    h = seq // 2
    return lax.broadcasted_iota(jnp.int32, (h, h), 0) <= lax.broadcasted_iota(jnp.int32, (h, h), 1)


def col(start, width):
    return pl.ds(pl.multiple_of(start, LANES), width)


KV_UNROLL = 2


def attn_fwd_body(kv_heads, rep, aliased, *refs):
    if aliased:
        refs = refs[:5] + refs[6:]
    qkv_ref, cos_ref, sin_ref, qn_ref, kn_ref, out_ref = refs
    cos_t, sin_t = cos_ref[...], sin_ref[...]
    q_gain, k_gain = qn_ref[...], kn_ref[...]
    tri = causal_by_key(qkv_ref.shape[0])
    h = tri.shape[0]
    k_base = kv_heads * rep * LANES
    v_base = k_base + kv_heads * LANES

    def per_kv(it, carry):
        for step in range(KV_UNROLL):
            g = it * KV_UNROLL + step
            k_rot, _, _ = head_prep(qkv_ref[:, col(k_base + g * LANES, LANES)], k_gain, cos_t, sin_t)
            v_raw = qkv_ref[:, col(v_base + g * LANES, LANES)]
            for r in range(rep):
                q_rot, _, _ = head_prep(qkv_ref[:, col((g * rep + r) * LANES, LANES)], q_gain, cos_t, sin_t)
                p_ll, p_lh, p_hh = [p.astype(BF16) for p in probs_by_key(q_rot, k_rot, tri)]
                at = col((r * kv_heads + g) * LANES, LANES)
                out_ref[:h, at] = dot_tn(p_ll, v_raw[:h]).astype(BF16)
                out_ref[h:, at] = dot_tn(jnp.concatenate([p_lh, p_hh], axis=0), v_raw).astype(BF16)
        return carry

    lax.fori_loop(0, kv_heads // KV_UNROLL, per_kv, 0)


def attn_bwd_body(kv_heads, rep, n_lead, lead_ref, tail_ref, do_ref, cos_ref, sin_ref, qn_ref, kn_ref, dqkv_ref, dqn_ref, dkn_ref):
    cos_t, sin_t = cos_ref[...], sin_ref[...]
    q_gain, k_gain = qn_ref[...], kn_ref[...]
    tri = causal_by_key(do_ref.shape[0])
    h = tri.shape[0]
    k_base = kv_heads * rep * LANES
    v_base = k_base + kv_heads * LANES
    scale = LANES ** -0.5

    @pl.when(pl.program_id(0) == 0)
    def _():
        dqn_ref[...] = jnp.zeros(dqn_ref.shape, F32)
        dkn_ref[...] = jnp.zeros(dkn_ref.shape, F32)

    def one_seq(qkv_ref):
        def one_kv(g, dqn, dkn):
            k_at = col(k_base + g * LANES, LANES)
            v_at = col(v_base + g * LANES, LANES)
            k_rot, k_normed, k_inv = head_prep(qkv_ref[:, k_at], k_gain, cos_t, sin_t)
            v_raw = qkv_ref[:, v_at]
            dk_l, dk_h, dv_l, dv_h = [], [], [], []
            for r in range(rep):
                at = col((g * rep + r) * LANES, LANES)
                q_rot, q_normed, q_inv = head_prep(qkv_ref[:, at], q_gain, cos_t, sin_t)
                grad_o = do_ref[:, col((r * kv_heads + g) * LANES, LANES)]
                p_ll, p_lh, p_hh = probs_by_key(q_rot, k_rot, tri)
                g_top = dot_nt(v_raw[:h], grad_o)
                g_ll, g_lh = g_top[:, :h], g_top[:, h:]
                g_hh = dot_nt(v_raw[h:], grad_o[h:])
                t_l = jnp.sum(g_ll * p_ll, axis=0, keepdims=True)
                t_h = jnp.sum(g_lh * p_lh, axis=0, keepdims=True) + jnp.sum(g_hh * p_hh, axis=0, keepdims=True)
                s_ll = (p_ll * ((g_ll - t_l) * scale)).astype(BF16)
                s_lh = (p_lh * ((g_lh - t_h) * scale)).astype(BF16)
                s_hh = (p_hh * ((g_hh - t_h) * scale)).astype(BF16)
                dv_l.append(dot_nn(jnp.concatenate([p_ll.astype(BF16), p_lh.astype(BF16)], axis=1), grad_o))
                dv_h.append(dot_nn(p_hh.astype(BF16), grad_o[h:]))
                dk_l.append(dot_nn(jnp.concatenate([s_ll, s_lh], axis=1), q_rot))
                dk_h.append(dot_nn(s_hh, q_rot[h:]))
                dq = jnp.concatenate([dot_tn(s_ll, k_rot[:h]), dot_tn(jnp.concatenate([s_lh, s_hh], axis=0), k_rot)], axis=0)
                dq_raw, gain_part = head_prep_bwd(dq, q_normed, q_inv, q_gain, cos_t, sin_t)
                dqn = dqn + gain_part
                dqkv_ref[:, at] = dq_raw
            dk = jnp.concatenate([sum(dk_l[1:], dk_l[0]), sum(dk_h[1:], dk_h[0])], axis=0)
            dk_raw, gain_part = head_prep_bwd(dk, k_normed, k_inv, k_gain, cos_t, sin_t)
            dkn = dkn + gain_part
            dqkv_ref[:, k_at] = dk_raw
            dqkv_ref[:h, v_at] = sum(dv_l[1:], dv_l[0]).astype(BF16)
            dqkv_ref[h:, v_at] = sum(dv_h[1:], dv_h[0]).astype(BF16)
            return dqn, dkn

        def per_kv(it, carry):
            for step in range(KV_UNROLL):
                carry = one_kv(it * KV_UNROLL + step, *carry)
            return carry

        zero = jnp.zeros((1, LANES), F32)
        dqn, dkn = lax.fori_loop(0, kv_heads // KV_UNROLL, per_kv, (zero, zero))
        dqn_ref[0:1, :] += dqn
        dkn_ref[0:1, :] += dkn

    @pl.when(pl.program_id(0) < n_lead)
    def _():
        one_seq(lead_ref)

    @pl.when(pl.program_id(0) >= n_lead)
    def _():
        one_seq(tail_ref)


def attn_fwd(qkv, cos_t, sin_t, q_gain, k_gain, n_seq, seq, kv_heads, rep, first, into):
    tokens, width = qkv.shape
    q_width = kv_heads * rep * LANES
    own = lambda w: pl.BlockSpec((seq, w), lambda b: (b, 0))
    shifted = lambda w: pl.BlockSpec((seq, w), lambda b: (b + first, 0))
    one = lambda r, w: pl.BlockSpec((r, w), lambda b: (0, 0))
    in_specs = [own(width), shifted(LANES), shifted(LANES), one(1, LANES), one(1, LANES)]
    args = (qkv, cos_t, sin_t, q_gain, k_gain)
    aliases = {}
    if into is not None:
        in_specs.append(pl.BlockSpec(memory_space=pl.ANY))
        args += (into,)
        aliases = {5: 0}
    return pl.pallas_call(
        functools.partial(attn_fwd_body, kv_heads, rep, into is not None),
        grid=(tokens // seq,),
        in_specs=in_specs,
        out_specs=shifted(q_width),
        out_shape=jax.ShapeDtypeStruct((n_seq * seq, q_width), BF16),
        input_output_aliases=aliases,
        compiler_params=pltpu.CompilerParams(dimension_semantics=("arbitrary",), vmem_limit_bytes=32 * 1024 * 1024),
        cost_estimate=pl.CostEstimate(flops=25_000_000_000, bytes_accessed=tokens * (width + q_width) * 2, transcendentals=4_200_000),
        name="attn_fwd",
    )(*args)


def attn_bwd(lead, tail, grad_o, cos_t, sin_t, q_gain, k_gain, seq, kv_heads, rep):
    tokens, q_width = grad_o.shape
    width = lead.shape[1]
    n_lead = lead.shape[0] // seq
    row = lambda w: pl.BlockSpec((seq, w), lambda b: (b, 0))
    one = lambda r, w: pl.BlockSpec((r, w), lambda b: (0, 0))
    lead_spec = pl.BlockSpec((seq, width), lambda b: (jnp.minimum(b, n_lead - 1), 0))
    tail_spec = pl.BlockSpec((seq, width), lambda b: (jnp.maximum(b - n_lead, 0), 0))
    return pl.pallas_call(
        functools.partial(attn_bwd_body, kv_heads, rep, n_lead),
        grid=(tokens // seq,),
        in_specs=[lead_spec, tail_spec, row(q_width), row(LANES), row(LANES), one(1, LANES), one(1, LANES)],
        out_specs=[row(width), one(SUBL, LANES), one(SUBL, LANES)],
        out_shape=[jax.ShapeDtypeStruct((tokens, width), BF16), jax.ShapeDtypeStruct((SUBL, LANES), F32), jax.ShapeDtypeStruct((SUBL, LANES), F32)],
        compiler_params=pltpu.CompilerParams(dimension_semantics=("arbitrary",), vmem_limit_bytes=40 * 1024 * 1024),
        cost_estimate=pl.CostEstimate(flops=100_000_000_000, bytes_accessed=tokens * (2 * width + q_width) * 2, transcendentals=8_400_000),
        name="attn_bwd",
    )(lead, tail, grad_o, cos_t, sin_t, q_gain, k_gain)


FF_TILE = 512
ROW_TILE = 1024
SUB_ROWS = 256


def swiglu_fwd_body(x_ref, w_ref, gu_ref, act_ref):
    for s in range(0, x_ref.shape[0], SUB_ROWS):
        rows = slice(s, s + SUB_ROWS)
        both = dot_nn(x_ref[rows, :], w_ref[...])
        gu_ref[rows, :] = both
        gate, up = both[:, :FF_TILE], both[:, FF_TILE:]
        act_ref[rows, :] = (gate * jax.nn.sigmoid(gate) * up).astype(BF16)


def swiglu_fwd(x, w_gu):
    tokens, dim = x.shape
    both = w_gu.shape[1]
    ff = both // 2
    return pl.pallas_call(
        swiglu_fwd_body,
        grid=(ff // FF_TILE, tokens // ROW_TILE),
        in_specs=[pl.BlockSpec((ROW_TILE, dim), lambda n, m: (m, 0)), pl.BlockSpec((dim, 2 * FF_TILE), lambda n, m: (0, n))],
        out_specs=[pl.BlockSpec((ROW_TILE, 2 * FF_TILE), lambda n, m: (m, n)), pl.BlockSpec((ROW_TILE, FF_TILE), lambda n, m: (m, n))],
        out_shape=[jax.ShapeDtypeStruct((tokens, both), F32), jax.ShapeDtypeStruct((tokens, ff), BF16)],
        compiler_params=pltpu.CompilerParams(dimension_semantics=("arbitrary", "arbitrary"), vmem_limit_bytes=40 * 1024 * 1024),
        cost_estimate=pl.CostEstimate(flops=2 * tokens * dim * both, bytes_accessed=tokens * both * 5, transcendentals=tokens * ff),
        name="swiglu_fwd",
    )(x, w_gu)


def swiglu_bwd_body(dy_ref, w_ref, gu_ref, dgu_ref):
    for s in range(0, dy_ref.shape[0], SUB_ROWS):
        rows = slice(s, s + SUB_ROWS)
        grad_act = dot_nt(dy_ref[rows, :], w_ref[...])
        gate, up = gu_ref[rows, :FF_TILE], gu_ref[rows, FF_TILE:]
        sig = jax.nn.sigmoid(gate)
        part = grad_act * sig
        dgu_ref[rows, :FF_TILE] = (part * up * (1.0 + gate * (1.0 - sig))).astype(BF16)
        dgu_ref[rows, FF_TILE:] = (part * gate).astype(BF16)


def swiglu_bwd(dy, w_down, gu):
    tokens, dim = dy.shape
    ff = w_down.shape[0]
    return pl.pallas_call(
        swiglu_bwd_body,
        grid=(ff // FF_TILE, tokens // ROW_TILE),
        in_specs=[pl.BlockSpec((ROW_TILE, dim), lambda n, m: (m, 0)), pl.BlockSpec((FF_TILE, dim), lambda n, m: (n, 0)), pl.BlockSpec((ROW_TILE, 2 * FF_TILE), lambda n, m: (m, n))],
        out_specs=pl.BlockSpec((ROW_TILE, 2 * FF_TILE), lambda n, m: (m, n)),
        out_shape=jax.ShapeDtypeStruct((tokens, 2 * ff), BF16),
        compiler_params=pltpu.CompilerParams(dimension_semantics=("arbitrary", "arbitrary"), vmem_limit_bytes=40 * 1024 * 1024),
        cost_estimate=pl.CostEstimate(flops=2 * tokens * dim * ff, bytes_accessed=tokens * ff * 12, transcendentals=tokens * ff),
        name="swiglu_bwd",
    )(dy, w_down, gu)


def norm_grad_body(as_rows, sub, g_ref, w_ref, x_ref, res_ref, gain_ref, *outs):
    gain = gain_ref[...]
    dgain_ref = outs[-1]

    @pl.when(pl.program_id(0) == 0)
    def _():
        dgain_ref[...] = jnp.zeros(dgain_ref.shape, F32)

    total = jnp.zeros(gain.shape, F32)
    for s in range(0, g_ref.shape[0], sub):
        rows = slice(s, s + sub)
        grad = dot_nt(g_ref[rows, :], w_ref[...])
        values = x_ref[rows, :].astype(F32)
        inv = lax.rsqrt(jnp.mean(values * values, axis=-1, keepdims=True) + NORM_EPS)
        normed = values * inv
        total = total + jnp.sum(grad * normed, axis=0, keepdims=True)
        scaled = grad * gain
        mean_term = jnp.mean(scaled * normed, axis=-1, keepdims=True)
        result = res_ref[rows, :].astype(F32) + inv * (scaled - normed * mean_term)
        if as_rows:
            for lane in range(SUBL):
                outs[0][pl.ds(s * SUBL + lane, sub, stride=SUBL), :] = result[:, lane * LANES:(lane + 1) * LANES]
        else:
            outs[0][rows, :] = result
            outs[1][rows, :] = result.astype(BF16)
    dgain_ref[0:1, :] += total


def norm_grad(g, w, x, residual, gain, as_rows):
    tokens, width = g.shape
    dim = w.shape[0]
    tile, sub = 512, 256
    row = lambda w: pl.BlockSpec((tile, w), lambda m: (m, 0))
    one = lambda r, w: pl.BlockSpec((r, w), lambda m: (0, 0))
    if as_rows:
        out_specs = [pl.BlockSpec((tile * SUBL, LANES), lambda m: (m, 0))]
        out_shape = [jax.ShapeDtypeStruct((tokens * SUBL, LANES), F32)]
    else:
        out_specs = [row(dim), row(dim)]
        out_shape = [jax.ShapeDtypeStruct((tokens, dim), F32), jax.ShapeDtypeStruct((tokens, dim), BF16)]
    return pl.pallas_call(
        functools.partial(norm_grad_body, as_rows, sub),
        grid=(tokens // tile,),
        in_specs=[row(width), pl.BlockSpec((dim, width), lambda m: (0, 0), pipeline_mode=pl.Buffered(1)), row(dim), row(dim), one(1, dim)],
        out_specs=out_specs + [one(SUBL, dim)],
        out_shape=out_shape + [jax.ShapeDtypeStruct((SUBL, dim), F32)],
        compiler_params=pltpu.CompilerParams(dimension_semantics=("arbitrary",), vmem_limit_bytes=VMEM_LIMIT),
        cost_estimate=pl.CostEstimate(flops=2 * tokens * dim * width, bytes_accessed=2 * tokens * width + 2 * dim * width + 12 * tokens * dim, transcendentals=0),
    )(g, w, x, residual, gain)


def norm_fwd(values):
    values_f = values.astype(F32)
    inv_rms = lax.rsqrt(jnp.mean(values_f * values_f, axis=-1, keepdims=True) + NORM_EPS)
    return values_f * inv_rms, inv_rms


def gather_rows(shard):
    return lax.all_gather(shard, AXIS_NAME, tiled=True)


def scatter_rows(grad):
    return lax.psum_scatter(grad, AXIS_NAME, scatter_dimension=0, tiled=True)


def side_by_side(gate, up):
    rows, ff = gate.shape
    tiles = ff // FF_TILE
    both = jnp.stack([gate.reshape(rows, tiles, FF_TILE), up.reshape(rows, tiles, FF_TILE)], axis=2)
    return both.reshape(rows, 2 * ff)


def take_apart(both):
    rows, width = both.shape
    parts = both.reshape(rows, width // (2 * FF_TILE), 2, FF_TILE)
    return parts[:, :, 0].reshape(rows, width // 2), parts[:, :, 1].reshape(rows, width // 2)


def solution(mesh):
    row_spec = P(AXIS_NAME, None)
    vec_spec = P(AXIS_NAME)
    full_spec = P(None)
    batch_spec = P(AXIS_NAME, None, None)
    weight_specs = (vec_spec, row_spec, row_spec, row_spec, full_spec, full_spec, row_spec, vec_spec, row_spec, row_spec, row_spec)

    def device_step(tokens, positions, table, attn_norm, w_query, w_key, w_value, q_norm, k_norm, w_out, mlp_norm, w_gate, w_up, w_down, dy_out):
        n_seq, seq = tokens.shape
        n_tok = n_seq * seq
        rows_local, dim = table.shape
        head = q_norm.shape[0]
        kv_heads = w_key.shape[1] // head
        rep = w_query.shape[1] // w_key.shape[1]
        q_width, kv_width = w_query.shape[1], w_key.shape[1]

        all_ids = gather_rows(tokens.reshape(-1))
        n_dev = all_ids.shape[0] // n_tok
        local_ids = all_ids - lax.axis_index(AXIS_NAME) * rows_local
        is_owner = (local_ids >= 0) & (local_ids < rows_local)
        owned_ids = jnp.where(is_owner, local_ids, rows_local)

        w_qkv = gather_rows(jnp.concatenate([w_query, w_key, w_value], axis=1))
        out_half = w_out.shape[0] // 2
        w_o = gather_rows(jnp.concatenate([w_out[:out_half], w_out[out_half:]], axis=1))
        n_lead = 5 * n_seq // 8
        lead_tok = n_lead * seq
        by_dev = owned_ids.reshape(n_dev, n_tok)
        ordered = jnp.concatenate([by_dev[:, :lead_tok].reshape(-1), by_dev[:, lead_tok:].reshape(-1)])
        picked_a, picked_b = table_gather(table, ordered, n_dev * lead_tok)
        x_a = scatter_rows(picked_a).reshape(lead_tok, dim)
        x_b = scatter_rows(picked_b).reshape(n_tok - lead_tok, dim)

        gu_local, down_local, norms_local, _ = lax.optimization_barrier((side_by_side(w_gate, w_up), w_down, jnp.stack([attn_norm, mlp_norm]), picked_b))
        w_gu = gather_rows(gu_local)
        w_d = gather_rows(down_local)
        norms = lax.all_gather(norms_local, AXIS_NAME, axis=1, tiled=True).astype(F32)
        attn_gain, mlp_gain = norms[0][None], norms[1][None]

        sid, perm = lax.sort([owned_ids, lax.iota(jnp.int32, all_ids.shape[0])], num_keys=1, is_stable=False)
        out_rows = block_of(rows_local, 300, SUBL)
        edges = lax.iota(jnp.int32, rows_local // out_rows + 1) * out_rows
        bst = jnp.sum((owned_ids[None, :] < edges[:, None]).astype(jnp.int32), axis=1)

        half = head // 2
        inv_freq = jnp.exp(jnp.arange(half, dtype=F32) * (-2.0 * math.log(ROPE_THETA) / head))
        angles = positions.reshape(-1).astype(F32)[:, None] * inv_freq
        cos_h, sin_h = jnp.cos(angles), jnp.sin(angles)
        cos_t = jnp.concatenate([cos_h, cos_h], axis=1)
        sin_t = jnp.concatenate([-sin_h, sin_h], axis=1)
        q_gain = q_norm.astype(F32)[None]
        k_gain = k_norm.astype(F32)[None]

        w_o = jnp.concatenate([w_o[:, :dim], w_o[:, dim:]], axis=0)

        def attn_norm_of(x_part):
            normed, _ = norm_fwd(x_part)
            return (normed * attn_gain).astype(BF16)

        qkv_a = dot_nn(attn_norm_of(x_a), w_qkv).astype(BF16)
        heads = attn_fwd(qkv_a, cos_t, sin_t, q_gain, k_gain, n_seq, seq, kv_heads, rep, 0, None)
        qkv_b = dot_nn(attn_norm_of(x_b), w_qkv).astype(BF16)
        heads = attn_fwd(qkv_b, cos_t, sin_t, q_gain, k_gain, n_seq, seq, kv_heads, rep, n_lead, heads)
        x_a, x_b, heads = lax.optimization_barrier((x_a, x_b, heads))
        x_emb = jnp.concatenate([x_a, x_b])
        hidden = (x_emb.astype(F32) + dot_nn(heads, w_o)).astype(BF16)
        normed2, _ = norm_fwd(hidden)
        mlp_in = (normed2 * mlp_gain).astype(BF16)
        gu, act = swiglu_fwd(mlp_in, w_gu)
        dy = dy_out.reshape(n_tok, dim)

        down_full, dy_later = lax.optimization_barrier((dot_tn(act, dy), dy))
        d_down = scatter_rows(down_full)
        dgu = swiglu_bwd(dy_later, w_d, gu)
        gu_full, dgu = lax.optimization_barrier((dot_tn(mlp_in, dgu), dgu))
        d_gu = scatter_rows(gu_full)
        grad_hidden, hidden_b, d_mlp_norm = norm_grad(dgu, w_gu, hidden, dy, mlp_gain, False)
        grad_heads = dot_nt(hidden_b, w_o).astype(BF16)
        dqkv, dqn, dkn = attn_bwd(qkv_a, qkv_b, grad_heads, cos_t, sin_t, q_gain, k_gain, seq, kv_heads, rep)
        grad_x, d_attn_norm = norm_grad(dqkv, w_qkv, x_emb, grad_hidden, attn_gain, True)
        grad_x = grad_x.reshape(n_tok, SUBL, LANES)
        grad_x, dqkv, act_later, hidden_later, x_later = lax.optimization_barrier((grad_x, dqkv, act, hidden_b, x_emb))
        all_rows = gather_rows(grad_x)
        d_out_full = dot_tn(heads, hidden_later)
        mid = d_out_full.shape[0] // 2
        d_qkvo = scatter_rows(jnp.concatenate([dot_tn(attn_norm_of(x_later), dqkv), d_out_full[:mid], d_out_full[mid:]], axis=1))
        layer_out = (hidden.astype(F32) + dot_nn(act_later, w_d)).astype(BF16)

        small = lax.psum(jnp.concatenate([d_attn_norm[0], d_mlp_norm[0], dqn[0], dkn[0]]), AXIS_NAME)
        shard_len = attn_norm.shape[0]
        at = lax.axis_index(AXIS_NAME) * shard_len
        d_attn_norm = lax.dynamic_slice(small, (at,), (shard_len,))
        d_mlp_norm = lax.dynamic_slice(small, (dim + at,), (shard_len,))
        d_q_norm = small[2 * dim:2 * dim + head]
        d_k_norm = small[2 * dim + head:]

        d_table = table_scatter(all_rows, perm, sid, bst, rows_local, out_rows)
        d_gate, d_up = take_apart(d_gu)
        cuts = [q_width, q_width + kv_width, q_width + 2 * kv_width, q_width + 2 * kv_width + dim]
        d_query, d_key, d_value, out_even, out_odd = jnp.split(d_qkvo, cuts, axis=1)
        d_out = jnp.concatenate([out_even, out_odd], axis=0)
        return (layer_out.reshape(n_seq, seq, dim), d_table, d_attn_norm, d_query, d_key, d_value, d_q_norm, d_k_norm, d_out, d_mlp_norm, d_gate, d_up, d_down)

    return jax.shard_map(device_step, mesh=mesh, in_specs=(row_spec, row_spec, row_spec) + weight_specs + (batch_spec,), out_specs=(batch_spec, row_spec) + weight_specs, check_vma=False)
```

time: 2690 us -> 1390 us (0.52)
  local copies, waits for them, and re-layouts: 686 us -> 66.5 us
  other arithmetic: 529 us -> 46 us
  Pallas kernels: 0 us -> 457 us
  blocking collectives: 426 us -> 46.1 us
  matrix products: 525 us -> 162 us
  waiting for transfers between devices: 492 us -> 591 us
    pallas_call x0 -> x9, Pallas kernels: none -> 457 us  [the longest x1 99.9 us: table_scatter(): pl.pallas_call(functools.partial(scatter_body, group, slots, out_rows), g...]
    gather x1 -> x0, local copies, waits for them, and re-layouts: 454 us -> none  [device_step(): jnp.take(table_shard, jnp.clip(local_ids, 0, rows_local - 1), axis=0)]
    all_gather x3 -> x2, blocking collectives: 402 us -> 23.5 us  [the longest x1 14.3 us: gather_rows(): return lax.all_gather(shard, AXIS_NAME, tiled=True)]
    dot_general x26 -> x9, matrix products: 498 us -> 162 us  [the longest x4 84.6 us: dot_tn(): lax.dot_general(a, b, (((0,), (0,)), ((), ())), preferred_element_type=F32)]
    scatter-add x3 -> x0, other arithmetic: 314 us -> none  [device_step(): jax.ops.segment_sum(all_rows, jnp.where(is_owner, local_ids, rows_local),...]
    all_gather x8 -> x5, waiting for transfers between devices: 167 us -> 338 us  [gather_rows(): return lax.all_gather(shard, AXIS_NAME, tiled=True)]
    mul x10 -> x0, local copies, waits for them, and re-layouts: 115 us -> none  [the longest x4 57.3 us: norm_fwd(): return (values_f * inv_rms, inv_rms)]
    reduce_scatter x8 -> x5, waiting for transfers between devices: 321 us -> 250 us  [scatter_rows(): return lax.psum_scatter(grad, AXIS_NAME, scatter_dimension=0, tiled=True)]
  transfers between devices with their start and end apart: 16 -> 10, of which waited for: 7 -> 5; matrix products, arithmetic and copies ran while one was open for 44% -> 16% of each run, Pallas kernels for 0% -> 31%
where the time goes in v1:
time: 1390 us; the launch traced here: 1380 us
  waiting for transfers between devices  591 us (43%)
  Pallas kernels  457 us (33%)
  matrix products  162 us (12%)
  local copies, waits for them, and re-layouts  66.5 us (5%)
  blocking collectives  46.1 us (3%)
  other arithmetic  46 us (3%)
  between operations  15.1 us (1%)
    all_gather x5, waiting for transfers between devices, gather_rows(): return lax.all_gather(shard, AXIS_NAME, tiled=True)  338 us
    reduce_scatter x5, waiting for transfers between devices, scatter_rows(): return lax.psum_scatter(grad, AXIS_NAME, scatter_dimension=0, tiled=True)  250 us
    pallas_call x1, Pallas kernels, table_scatter(): pl.pallas_call(functools.partial(scatter_body, group, slots, out_rows), g...  99.9 us
    dot_general x4, matrix products, dot_tn(): lax.dot_general(a, b, (((0,), (0,)), ((), ())), preferred_element_type=F32)  84.6 us
    pallas_call x1, Pallas kernels, attn_bwd(): pl.pallas_call(functools.partial(attn_bwd_body, kv_heads, rep, n_lead), g...  82.5 us
    pallas_call x2, Pallas kernels, norm_grad(): pl.pallas_call(functools.partial(norm_grad_body, as_rows, sub), grid=(tok...  72.5 us
    pallas_call x1, Pallas kernels, table_gather(): pl.pallas_call(functools.partial(gather_body, n_tab, n_lead, tab_rows, to...  67.4 us
    pallas_call x2, Pallas kernels, attn_fwd(): pl.pallas_call(functools.partial(attn_fwd_body, kv_heads, rep, into is no...  64.1 us
  transfers between devices with their start and end apart: 10, of which 5 were waited for; matrix products, arithmetic and copies ran while one was open for 16% of the time, Pallas kernels for 31%

profile of v1, /device:TPU:0, one launch (start us, length us, event | category | flops | bytes accessed | tf_op | source)
XLA Modules:
  0.0 1383.6 jit_solution(17053100383474955138)
XLA Ops:
  7.2 1.1 fusion.21
  8.3 0.8 pad_maximum_fusion.9
  9.2 0.7 copy.49
  9.9 14.3 %all_gather.21 = s32[16384]{0:T(1024)S(1)} all-gather(s32[2048]{0:T(1024)S(1)} %bitcast.76), channel_id=1, replica_groups=mesh['fsdp'=8] {'fsdp'}, dimensions={0}, use_global_device_ids=true | all-gather | bytes 73728 | tf_op jit(solution)/shard_map/all_gather | solution.py:479
  25.0 67.4 %table_gather.1 = (bf16[10240,8,128]{2,1,0:T(8,128)(2,1)}, bf16[6144,8,128]{2,1,0:T(8,128)(2,1)}) custom-call(s32[16384]{0:T(1024)} %pad_add_fusion.idx_ref, bf16[19008,1024]{1,0:T(8,128)(2,1)} %tab_ref.1), custom_call_target="tpu_custom_call" | custom-call | flops 70000001024 | bytes 72482816 | tf_op jit(solution)/shard_map/table_gather/pallas_call | solution.py:91
  92.4 0.9 copy-done.17
  93.5 1.0 pad_maximum_fusion.5
  95.2 0.8 copy-done.15
  97.0 1.5 copy.45
  98.5 2.1 reshape.114
  101.2 9.2 all_gather.22
  110.5 3.7 fusion.15
  114.8 5.5 fusion.19
  120.4 55.9 %reduce-scatter.8.cloned.1.call-done = bf16[768,8,128]{2,1,0:T(8,128)(2,1)} async-done(((bf16[6144,8,128]{2,1,0:T(8,128)(2,1)}), bf16[768,8,128]{2,1,0:T(8,128)(2,1)}) %reduce-scatter.8.cloned.1.call-update) | async-done | bytes 1572880 | tf_op jit(solution)/shard_map/reduce_scatter | solution.py:483
  176.3 2.9 multiply_reduce_fusion.1
  179.2 3.0 copy.64
  182.2 45.3 %all-gather.6.cloned.1.call-done.w_ref = bf16[1024,4096]{1,0:T(8,128)(2,1)} async-done(((bf16[128,4096]{1,0:T(8,128)(2,1)}), bf16[1024,4096]{1,0:T(8,128)(2,1)}) %all-gather.6.cloned.1.call-update) | async-done | bytes 8388624 | tf_op jit(solution)/shard_map/all_gather | solution.py:479
  227.4 12.7 convolution_convert_fusion.2.refs_0_.tail_ref
  240.2 119.3 %reduce-scatter.6.cloned.1.call-done = bf16[1280,8,128]{2,1,0:T(8,128)(2,1)} async-done(((bf16[10240,8,128]{2,1,0:T(8,128)(2,1)}), bf16[1280,8,128]{2,1,0:T(8,128)(2,1)}) %reduce-scatter.6.cloned.1.call-update) | async-done | bytes 2621456 | tf_op jit(solution)/shard_map/reduce_scatter | solution.py:483
  359.5 10.9 multiply_reduce_fusion
  370.4 17.9 %convolution_convert_fusion.refs_0_.lead_ref = bf16[1280,4096]{1,0:T(8,128)(2,1)} fusion(bf16[1024,4096]{1,0:T(8,128)(2,1)} %all-gather.6.cloned.1.call-done.w_ref, f32[1024]{0:T(1024)S(1)} %bitcast.82, f32[1280]{0:T(1024)S(1)} %add_rsqrt_fusion.2, bf16[160,8,8,128]{3,2,1,0:T(8,128)(2,1)} %bitcast.62), kind=kOutput, calls=%fused_computation.1 | convolution fusion | flops 10747904000 | bytes 21505024 | tf_op jit(solution)/shard_map/dot_general | solution.py:29
  388.3 5.9 copy-done.6
  394.2 39.8 %attn_fwd.2.refs_5_ = bf16[2048,2048]{1,0:T(8,128)(2,1)S(1)} custom-call(bf16[1280,4096]{1,0:T(8,128)(2,1)S(1)} %copy-done.6, f32[2048,128]{1,0:T(8,128)S(1)} %get-tuple-element.94.refs_1_.cos_ref, f32[2048,128]{1,0:T(8,128)S(1)} %get-tuple-element.95.refs_2_.sin_ref, f32[1,128]{1,0:T(1,128)S(1)} %get-tuple-element.97.refs_3_.qn_ref, ...), custom_call_target="tpu_custom_call" | custom-call | flops 24999999488 | bytes 15728640 | tf_op jit(solution)/shard_map/attn_fwd/pallas_call | solution.py:332
  434.7 24.3 %attn_fwd.3 = bf16[2048,2048]{1,0:T(8,128)(2,1)S(1)} custom-call(bf16[768,4096]{1,0:T(8,128)(2,1)S(1)} %bitcast.61, f32[2048,128]{1,0:T(8,128)S(1)} %get-tuple-element.94.refs_1_.cos_ref, f32[2048,128]{1,0:T(8,128)S(1)} %get-tuple-element.95.refs_2_.sin_ref, f32[1,128]{1,0:T(1,128)S(1)} %get-tuple-element.97.refs_3_.qn_ref, ...), custom_call_target="tpu_custom_call", output_to_operand_aliasing={{}: (5, {})} | custom-call | flops 24999999488 | bytes 9437184 | tf_op jit(solution)/shard_map/attn_fwd/pallas_call | solution.py:332
  459.2 2.3 copy-done.10
  461.7 1.4 copy-done.5
  463.1 0.7 copy-done.12
  463.8 11.8 fusion.3
  475.6 2.0 copy-done.11
  477.6 2.5 fusion.5.x_ref
  480.1 2.2 copy-done.1
  482.3 36.8 %swiglu_fwd.1 = (f32[2048,6144]{1,0:T(8,128)}, bf16[2048,3072]{1,0:T(8,128)(2,1)}) custom-call(bf16[2048,1024]{1,0:T(8,128)(2,1)S(1)} %copy-done.1, bf16[1024,6144]{1,0:T(8,128)(2,1)} %all-gather.10.cloned.1.call-done.w_ref), custom_call_target="tpu_custom_call" | custom-call | flops 25769803776 | bytes 62914560 | tf_op jit(solution)/shard_map/swiglu_fwd/pallas_call | solution.py:383
  519.1 18.1 %fusion.24 = f32[3072,1024]{1,0:T(8,128)} fusion(bf16[2048,3072]{1,0:T(8,128)(2,1)} %get-tuple-element.58, bf16[2048,1024]{1,0:T(8,128)(2,1)S(1)} %bitcast.58), kind=kOutput, calls=%fused_computation.68 | convolution fusion | flops 12884901888 | bytes 29360128 | tf_op jit(solution)/shard_map/dot_general | solution.py:25
  537.2 2.8 copy-done
  540.0 2.2 copy-done.4
  542.2 34.0 %swiglu_bwd.1.g_ref = bf16[2048,6144]{1,0:T(8,128)(2,1)} custom-call(bf16[2048,1024]{1,0:T(8,128)(2,1)S(1)} %bitcast.59, bf16[3072,1024]{1,0:T(8,128)(2,1)S(1)} %copy-done, f32[2048,6144]{1,0:T(8,128)} %get-tuple-element.52.gu_ref), custom_call_target="tpu_custom_call" | custom-call | flops 12884901888 | bytes 75497472 | tf_op jit(solution)/shard_map/swiglu_bwd/pallas_call | solution.py:409
  576.2 31.8 %fusion.25 = f32[1024,6144]{1,0:T(8,128)} fusion(bf16[2048,1024]{1,0:T(8,128)(2,1)S(1)} %copy-done.2, bf16[2048,6144]{1,0:T(8,128)(2,1)} %swiglu_bwd.1.g_ref), kind=kOutput, calls=%fused_computation.69 | convolution fusion | flops 25769803776 | bytes 54525952 | tf_op jit(solution)/shard_map/dot_general | solution.py:25
  608.1 42.4 %shard_map.246 = (f32[2048,1024]{1,0:T(8,128)}, bf16[2048,1024]{1,0:T(8,128)(2,1)}, f32[8,1024]{1,0:T(8,128)}) custom-call(bf16[2048,6144]{1,0:T(8,128)(2,1)} %swiglu_bwd.1.g_ref, bf16[1024,6144]{1,0:T(8,128)(2,1)} %all-gather.10.cloned.1.call-done.w_ref, bf16[2048,1024]{1,0:T(8,128)(2,1)} %copy-done.11, bf16[2048,1024]{1,0:T(8,128)(2,1)} %bitcast.57, ...), custom_call_target="tpu_custom_call" | custom-call | flops 25769803776 | bytes 62914560 | tf_op jit(solution)/shard_map/pallas_call | solution.py:461
  650.5 14.3 %convolution_convert_fusion.1.do_ref = bf16[2048,2048]{1,0:T(8,128)(2,1)} fusion(bf16[2048,1024]{1,0:T(8,128)(2,1)} %get-tuple-element.68, bf16[1024,1024]{1,0:T(8,128)(2,1)} %get-tuple-element.76, bf16[1024,1024]{1,0:T(8,128)(2,1)} %get-tuple-element.75), kind=kOutput, calls=%fused_computation.15 | convolution fusion | flops 8602517504 | bytes 16777216 | tf_op jit(solution)/shard_map/dot_general | solution.py:21
  664.9 3.0 copy-done.7
  667.9 82.5 %attn_bwd.1 = (bf16[2048,4096]{1,0:T(8,128)(2,1)}, f32[8,128]{1,0:T(8,128)S(1)}, f32[8,128]{1,0:T(8,128)S(1)}) custom-call(bf16[1280,4096]{1,0:T(8,128)(2,1)} %convolution_convert_fusion.refs_0_.lead_ref, bf16[768,4096]{1,0:T(8,128)(2,1)S(1)} %copy-done.7, bf16[2048,2048]{1,0:T(8,128)(2,1)} %convolution_convert_fusion.1.do_ref, ...), custom_call_target="tpu_custom_call" | custom-call | flops 99999997952 | bytes 41943040 | tf_op jit(solution)/shard_map/attn_bwd/pallas_call | solution.py:353
  750.4 30.1 %shard_map.247 = (f32[16384,128]{1,0:T(8,128)}, f32[8,1024]{1,0:T(8,128)}) custom-call(bf16[2048,4096]{1,0:T(8,128)(2,1)} %get-tuple-element.67.g_ref, bf16[1024,4096]{1,0:T(8,128)(2,1)} %all-gather.6.cloned.1.call-done.w_ref, bf16[2048,1024]{1,0:T(8,128)(2,1)} %copy-done.8, f32[2048,1024]{1,0:T(8,128)} %get-tuple-element.56.res_ref, f32[1,1024]{1,0:T(1,128)} %copy-done.22), custom_call_target="tpu_custom_call" | custom-call | flops 17179869184 | bytes 50331648 | tf_op jit(solution)/shard_map/pallas_call | solution.py:461
  780.5 3.2 fusion
  784.0 12.0 fusion.26
  796.0 0.8 fusion.18
  796.8 22.7 %fusion.7 = f32[1024,4096]{1,0:T(8,128)S(1)} fusion(bf16[2048,4096]{1,0:T(8,128)(2,1)} %get-tuple-element.67.g_ref, bf16[2048,1024]{1,0:T(8,128)(2,1)} %copy-done.8, f32[1024]{0:T(1024)S(1)} %bitcast.83, f32[2048]{0:T(1024)S(1)} %add_rsqrt_fusion), kind=kOutput, calls=%fused_computation.20 | convolution fusion | flops 17188257792 | bytes 37761024 | tf_op jit(solution)/shard_map/dot_general | solution.py:25
  819.5 11.2 pad_maximum_fusion
  830.8 0.7 all-gather.14.cloned.1.call-update
  832.3 6.4 sort.15
  838.8 0.8 convert_reduce_fusion.bst_ref
  839.6 0.8 slice.63
  840.4 0.8 slice.62
  841.2 22.6 %psum.7 = f32[2304]{0:T(1024)S(1)} all-reduce(f32[2304]{0:T(1024)S(1)} %pad_maximum_fusion.10), channel_id=1, replica_groups=mesh['fsdp'=8] {'fsdp'}, use_global_device_ids=true, to_apply=%region_7.8 | all-reduce | flops 2304 | bytes 18432 | tf_op jit(solution)/shard_map/psum | solution.py:587
  864.4 20.2 %fusion.6 = bf16[2048,1024]{1,0:T(8,128)(2,1)} fusion(bf16[2048,1024]{1,0:T(8,128)(2,1)} %copy-done.11, bf16[2048,3072]{1,0:T(8,128)(2,1)} %get-tuple-element.58, bf16[3072,1024]{1,0:T(8,128)(2,1)} %all-gather.12.cloned.1.call-done.w_ref), kind=kOutput, calls=%fused_computation.13 | convolution fusion | flops 12891193344 | bytes 27262976 | tf_op jit(solution)/shard_map/dot_general | solution.py:29
  884.6 4.2 reshape.118
  888.8 8.9 slice_reduce_fusion
  897.8 2.4 copy.54
  900.1 2.4 copy.53
  902.5 75.0 %reduce-scatter.10.cloned.1.call-done = f32[128,6144]{1,0:T(8,128)} async-done(((f32[1024,6144]{1,0:T(8,128)}), f32[128,6144]{1,0:T(8,128)}) %reduce-scatter.10.cloned.1.call-update) | async-done | bytes 3145744 | tf_op jit(solution)/shard_map/reduce_scatter | solution.py:483
  977.5 2.3 split.20
  979.8 2.7 fusion.20
  982.5 1.0 pad_maximum_fusion.8
  983.5 293.0 %all-gather.14.cloned.1.call-done.rows_ref = f32[16384,8,128]{2,1,0:T(8,128)} async-done(((f32[2048,8,128]{2,1,0:T(8,128)}), f32[16384,8,128]{2,1,0:T(8,128)}) %all-gather.14.cloned.1.call-update) | async-done | bytes 67108880 | tf_op jit(solution)/shard_map/all_gather | solution.py:479
  1276.5 99.9 %table_scatter.1 = f32[19008,1024]{1,0:T(8,128)} custom-call(s32[16384]{0:T(1024)S(1)} %get-tuple-element.59.perm_ref, s32[16384]{0:T(1024)S(1)} %get-tuple-element.60.sid_ref, s32[67]{0:T(128)S(1)} %convert_reduce_fusion.bst_ref, f32[16384,8,128]{2,1,0:T(8,128)} %all-gather.14.cloned.1.call-done.rows_ref), custom_call_target="tpu_custom_call" | custom-call | flops 70000001024 | bytes 144965632 | tf_op jit(solution)/shard_map/table_scatter/pallas_call | solution.py:166
  (106 shorter events, 6.7 us)
Async XLA Ops:
  7.2 107.7 %all-gather.8.cloned.1.call-start = ((), (), s32[]{:S(2)}) async-start(), calls=%async_computation.8 | async-start | bytes 4718592 | tf_op jit(solution)/shard_map/all_gather | solution.py:479
  9.1 167.1 %reduce-scatter.8.cloned.1.call-start = ((), (), s32[]{:S(2)}) async-start(), calls=%async_computation.6 | async-start | bytes 14155776 | tf_op jit(solution)/shard_map/reduce_scatter | solution.py:483
  24.3 68.1 %copy-start.13 = (s32[16384]{0:T(1024)}, s32[16384]{0:T(1024)S(1)}, u32[]{:S(2)}) copy-start(s32[16384]{0:T(1024)S(1)} %and_select_fusion) | copy-start | bytes 196612
  92.3 1.0 copy-start.17
  92.3 1.1 copy-start.18
  92.4 1.2 copy-start.19
  92.4 135.0 %all-gather.6.cloned.1.call-start = ((), (), s32[]{:S(2)}) async-start(), calls=%async_computation.7 | async-start | bytes 9437184 | tf_op jit(solution)/shard_map/all_gather | solution.py:479
  94.6 264.9 %reduce-scatter.6.cloned.1.call-start = ((), (), s32[]{:S(2)}) async-start(), calls=%async_computation.5 | async-start | bytes 23592960 | tf_op jit(solution)/shard_map/reduce_scatter | solution.py:483
  94.6 1.4 copy-start.15
  94.7 1.7 copy-start.16
  95.2 384.9 %all-gather.10.cloned.1.call-start = ((), (), s32[]{:S(2)}) async-start(), calls=%async_computation.9 | async-start | bytes 14155776 | tf_op jit(solution)/shard_map/all_gather | solution.py:479
  96.8 3.8 copy-start.26
  96.8 3.7 copy-start.27
  97.0 4.3 copy-start.21
  97.0 13.5 copy-start.24
  97.0 13.5 copy-start.25
  100.6 436.6 %all-gather.12.cloned.1.call-start = ((), (), s32[]{:S(2)}) async-start(), calls=%async_computation.10 | async-start | bytes 7077888 | tf_op jit(solution)/shard_map/all_gather | solution.py:479
  101.2 783.5 %reduce-scatter.12.cloned.1.call-start = ((), (), s32[]{:S(2)}) async-start(), calls=%async_computation.13 | async-start | bytes 28311552 | tf_op jit(solution)/shard_map/reduce_scatter | solution.py:483
  110.4 260.0 %copy-start.22 = (f32[1,1024]{1,0:T(1,128)}, f32[1,1024]{1,0:T(1,128)S(1)}, u32[]{:S(2)}) copy-start(f32[1,1024]{1,0:T(1,128)S(1)} %get-tuple-element.91.gain_ref) | copy-start | bytes 12292
  110.5 365.2 %copy-start.20 = (f32[1,1024]{1,0:T(1,128)}, f32[1,1024]{1,0:T(1,128)S(1)}, u32[]{:S(2)}) copy-start(f32[1,1024]{1,0:T(1,128)S(1)} %get-tuple-element.90.gain_ref) | copy-start | bytes 12292
  370.4 64.2 %slice-start = ((s8[6291456]{0:T(1024)(128)(4,1)}), s8[4194304]{0:T(1024)(128)(4,1)S(1)}, s32[]{:S(2)}) async-start(s8[6291456]{0:T(1024)(128)(4,1)} %bitcast.60), calls=%async_computation.15 | async-start | bytes 8388608
  388.3 5.9 copy-start.6
  394.2 39.8 %copy-start.9 = (bf16[1280,8,128]{2,1,0:T(8,128)(2,1)S(1)}, bf16[1280,8,128]{2,1,0:T(8,128)(2,1)}, u32[]{:S(2)}) copy-start(bf16[1280,8,128]{2,1,0:T(8,128)(2,1)} %reduce-scatter.6.cloned.1.call-done) | copy-start | bytes 7864324
  394.2 40.5 %slice-start.1 = ((s8[6291456]{0:T(1024)(128)(4,1)}), s8[2097152]{0:T(1024)(128)(4,1)S(1)}, s32[]{:S(2)}) async-start(s8[6291456]{0:T(1024)(128)(4,1)} %bitcast.60), calls=%async_computation.16 | async-start | bytes 4194304
  459.0 4.1 copy-start.5
  459.0 2.6 copy-start.10
  459.0 4.8 copy-start.12
  461.7 13.9 %copy-start.8 = (bf16[2048,1024]{1,0:T(8,128)(2,1)}, bf16[2048,1024]{1,0:T(8,128)(2,1)S(1)}, u32[]{:S(2)}) copy-start(bf16[2048,1024]{1,0:T(8,128)(2,1)S(1)} %constant_dynamic-update-slice_fusion.x_ref) | copy-start | bytes 12582916
  475.6 2.0 copy-start.11
  480.1 2.2 copy-start.1
  482.3 36.8 %copy-start.3 = (bf16[8,256,1024]{2,1,0:T(8,128)(2,1)S(1)}, bf16[8,256,1024]{2,1,0:T(8,128)(2,1)}, u32[]{:S(2)}) copy-start(bf16[8,256,1024]{2,1,0:T(8,128)(2,1)} %param.29) | copy-start | bytes 12582916
  537.2 2.8 copy-start
  540.0 2.2 copy-start.4
  542.2 34.0 %copy-start.2 = (bf16[2048,1024]{1,0:T(8,128)(2,1)S(1)}, bf16[2048,1024]{1,0:T(8,128)(2,1)}, u32[]{:S(2)}) copy-start(bf16[2048,1024]{1,0:T(8,128)(2,1)} %fusion.5.x_ref) | copy-start | bytes 12582916
  608.0 369.4 %reduce-scatter.10.cloned.1.call-start = ((), (), s32[]{:S(2)}) async-start(), calls=%async_computation.12 | async-start | bytes 28311552 | tf_op jit(solution)/shard_map/reduce_scatter | solution.py:483
  664.9 3.0 copy-start.7
  780.5 3.4 copy-start.28
  795.9 0.9 copy-start.23
  830.7 445.8 %all-gather.14.cloned.1.call-start = ((), (), s32[]{:S(2)}) async-start(), calls=%async_computation.11 | async-start | bytes 75497472 | tf_op jit(solution)/shard_map/all_gather | solution.py:479
  831.5 0.9 copy-start.14
  831.5 544.9 %reduce-scatter.14.cloned.1.call-start = ((), (), s32[]{:S(2)}) async-start(), calls=%async_computation.14 | async-start | bytes 14155776 | tf_op jit(solution)/shard_map/reduce_scatter | solution.py:483
Sparse Core Ops, SparseCore 0:
  10.4 34.1 all-gather.7
  92.5 83.7 reduce-scatter.7
  178.7 48.6 all-gather.5
  231.4 128.0 reduce-scatter.5
  361.7 66.4 all-gather.9
  429.9 39.8 all-gather.11
  608.2 147.6 reduce-scatter.11
  830.8 146.5 reduce-scatter.9
  979.3 297.1 all-gather.13
  1280.3 83.9 reduce-scatter.13

commit v2 on v1

--- a/solution.py
+++ b/solution.py
@@ -37,7 +37,8 @@
     return best
 
 
-def gather_body(n_tab, n_lead, tab_rows, tok_rows, idx_ref, tab_ref, lead_ref, tail_ref, store, stage):
+def gather_body(n_tab, starts, tab_rows, tok_rows, idx_ref, tab_ref, *refs):
+    out_refs, (store, stage) = refs[:-2], refs[-2:]
     step = pl.program_id(0)
 
     @pl.when(step == 0)
@@ -63,37 +64,32 @@
 
         lax.fori_loop(0, tok_rows // unroll, loop, 0)
 
-    @pl.when((step >= n_tab) & (step < n_tab + n_lead))
-    def _():
-        copy_rows(lead_ref)
-
-    @pl.when(step >= n_tab + n_lead)
-    def _():
-        copy_rows(tail_ref)
-
-
-def table_gather(table, idx, lead):
+    for k, out_ref in enumerate(out_refs):
+        @pl.when((step >= n_tab + starts[k]) & (step < n_tab + starts[k + 1]))
+        def _(out_ref=out_ref):
+            copy_rows(out_ref)
+
+
+def table_gather(table, idx, counts):
     rows, width = table.shape
-    total = idx.shape[0]
     tab_rows = block_of(rows, 640, 16)
     n_tab = rows // tab_rows
     tok_rows = 512
-    n_lead, n_tail = lead // tok_rows, (total - lead) // tok_rows
-    out_block = (tok_rows, SUBL, LANES)
+    starts = [sum(counts[:k]) // tok_rows for k in range(len(counts) + 1)]
+    out_spec = lambda lo, hi: pl.BlockSpec((tok_rows, SUBL, LANES), lambda s, ids: (jnp.clip(s - n_tab - lo, 0, hi - lo - 1), 0, 0))
     grid_spec = pltpu.PrefetchScalarGridSpec(
         num_scalar_prefetch=1,
-        grid=(n_tab + n_lead + n_tail,),
+        grid=(n_tab + starts[-1],),
         in_specs=[pl.BlockSpec((tab_rows, width), lambda s, ids: (jnp.minimum(s, n_tab - 1), 0))],
-        out_specs=[pl.BlockSpec(out_block, lambda s, ids: (jnp.clip(s - n_tab, 0, n_lead - 1), 0, 0)),
-                   pl.BlockSpec(out_block, lambda s, ids: (jnp.clip(s - n_tab - n_lead, 0, n_tail - 1), 0, 0))],
+        out_specs=[out_spec(lo, hi) for lo, hi in zip(starts, starts[1:])],
         scratch_shapes=[pltpu.VMEM((rows + 8, SUBL, LANES), BF16), pltpu.VMEM((tab_rows * SUBL, LANES), F32)],
     )
     return pl.pallas_call(
-        functools.partial(gather_body, n_tab, n_lead, tab_rows, tok_rows),
+        functools.partial(gather_body, n_tab, starts, tab_rows, tok_rows),
         grid_spec=grid_spec,
-        out_shape=[jax.ShapeDtypeStruct((n * tok_rows, SUBL, LANES), BF16) for n in (n_lead, n_tail)],
+        out_shape=[jax.ShapeDtypeStruct((n, SUBL, LANES), BF16) for n in counts],
         compiler_params=pltpu.CompilerParams(dimension_semantics=("arbitrary",), vmem_limit_bytes=VMEM_LIMIT),
-        cost_estimate=pl.CostEstimate(flops=70_000_000_000, bytes_accessed=rows * width * 2 + total * width * 2, transcendentals=0),
+        cost_estimate=pl.CostEstimate(flops=70_000_000_000, bytes_accessed=rows * width * 2 + sum(counts) * width * 2, transcendentals=0),
         name="table_gather",
     )(idx, table)
 
@@ -483,6 +479,21 @@
     return lax.psum_scatter(grad, AXIS_NAME, scatter_dimension=0, tiled=True)
 
 
+def partner_sum(keep, send):
+    n_dev = lax.axis_size(AXIS_NAME)
+    return keep + lax.ppermute(send, AXIS_NAME, [(i, i ^ 1) for i in range(n_dev)])
+
+
+def scatter_rows_by_chip(value):
+    n_dev = lax.axis_size(AXIS_NAME)
+    groups = [list(range(core, n_dev, 2)) for core in range(2)]
+    return lax.psum_scatter(value, AXIS_NAME, scatter_dimension=0, tiled=True, axis_index_groups=groups)
+
+
+def pick_block(value, index, dim):
+    return lax.dynamic_index_in_dim(value, index, dim, keepdims=False)
+
+
 def side_by_side(gate, up):
     rows, ff = gate.shape
     tiles = ff // FF_TILE
@@ -520,20 +531,26 @@
 
         w_qkv = gather_rows(jnp.concatenate([w_query, w_key, w_value], axis=1))
         out_half = w_out.shape[0] // 2
-        w_o = gather_rows(jnp.concatenate([w_out[:out_half], w_out[out_half:]], axis=1))
+        gain_cols = jnp.pad(jnp.stack([attn_norm, mlp_norm], axis=1), ((0, 0), (0, LANES - 2)))
+        w_o = gather_rows(jnp.concatenate([w_out[:out_half], w_out[out_half:], gain_cols], axis=1))
         n_lead = 5 * n_seq // 8
         lead_tok = n_lead * seq
-        by_dev = owned_ids.reshape(n_dev, n_tok)
-        ordered = jnp.concatenate([by_dev[:, :lead_tok].reshape(-1), by_dev[:, lead_tok:].reshape(-1)])
-        picked_a, picked_b = table_gather(table, ordered, n_dev * lead_tok)
-        x_a = scatter_rows(picked_a).reshape(lead_tok, dim)
-        x_b = scatter_rows(picked_b).reshape(n_tok - lead_tok, dim)
-
-        gu_local, down_local, norms_local, _ = lax.optimization_barrier((side_by_side(w_gate, w_up), w_down, jnp.stack([attn_norm, mlp_norm]), picked_b))
+        core = lax.axis_index(AXIS_NAME) & 1
+        n_chip = n_dev // 2
+        by_dev = owned_ids.reshape(n_chip, 2, n_tok)
+        keep_ids, send_ids = pick_block(by_dev, core, 1), pick_block(by_dev, 1 - core, 1)
+        parts = [send_ids[:, :lead_tok], keep_ids[:, :lead_tok], send_ids[:, lead_tok:], keep_ids[:, lead_tok:]]
+        send_a, keep_a, send_b, keep_b = table_gather(table, jnp.concatenate([p.reshape(-1) for p in parts]), [p.size for p in parts])
+        sum_a = partner_sum(keep_a, send_a)
+        x_a = scatter_rows_by_chip(sum_a).reshape(lead_tok, dim)
+        sum_b = partner_sum(keep_b, send_b)
+        x_b = scatter_rows_by_chip(sum_b).reshape(n_tok - lead_tok, dim)
+
+        gu_local, down_local, _ = lax.optimization_barrier((side_by_side(w_gate, w_up), w_down, keep_b))
         w_gu = gather_rows(gu_local)
         w_d = gather_rows(down_local)
-        norms = lax.all_gather(norms_local, AXIS_NAME, axis=1, tiled=True).astype(F32)
-        attn_gain, mlp_gain = norms[0][None], norms[1][None]
+        gains = w_o[:, 2 * dim:2 * dim + 2].astype(F32).T
+        attn_gain, mlp_gain = gains[0:1], gains[1:2]
 
         sid, perm = lax.sort([owned_ids, lax.iota(jnp.int32, all_ids.shape[0])], num_keys=1, is_stable=False)
         out_rows = block_of(rows_local, 300, SUBL)
@@ -549,7 +566,7 @@
         q_gain = q_norm.astype(F32)[None]
         k_gain = k_norm.astype(F32)[None]
 
-        w_o = jnp.concatenate([w_o[:, :dim], w_o[:, dim:]], axis=0)
+        w_o = jnp.concatenate([w_o[:, :dim], w_o[:, dim:2 * dim]], axis=0)
 
         def attn_norm_of(x_part):
             normed, _ = norm_fwd(x_part)
@@ -581,7 +598,10 @@
         all_rows = gather_rows(grad_x)
         d_out_full = dot_tn(heads, hidden_later)
         mid = d_out_full.shape[0] // 2
-        d_qkvo = scatter_rows(jnp.concatenate([dot_tn(attn_norm_of(x_later), dqkv), d_out_full[:mid], d_out_full[mid:]], axis=1))
+        qkvo_full = jnp.concatenate([dot_tn(attn_norm_of(x_later), dqkv), d_out_full[:mid], d_out_full[mid:]], axis=1)
+        qkvo_full = qkvo_full.reshape(n_chip, 2, -1, qkvo_full.shape[1])
+        qkvo_sum = partner_sum(pick_block(qkvo_full, core, 1), pick_block(qkvo_full, 1 - core, 1))
+        d_qkvo = scatter_rows_by_chip(qkvo_sum.reshape(-1, qkvo_sum.shape[-1]))
         layer_out = (hidden.astype(F32) + dot_nn(act_later, w_d)).astype(BF16)
 
         small = lax.psum(jnp.concatenate([d_attn_norm[0], d_mlp_norm[0], dqn[0], dkn[0]]), AXIS_NAME)

time: 1390 us -> 1560 us (1.12)
  waiting for transfers between devices: 591 us -> 718 us
  other arithmetic: 46 us -> 76.4 us
    reduce_scatter x0 -> x3, waiting for transfers between devices: none -> 525 us  [scatter_rows_by_chip(): lax.psum_scatter(value, AXIS_NAME, scatter_dimension=0, tiled=True, axis_...]
    all_gather x5, waiting for transfers between devices: 338 us -> 0.03 us  [gather_rows(): return lax.all_gather(shard, AXIS_NAME, tiled=True)]
    reduce_scatter x5 -> x2, waiting for transfers between devices: 250 us -> 145 us  [scatter_rows(): return lax.psum_scatter(grad, AXIS_NAME, scatter_dimension=0, tiled=True)]
    ppermute x0 -> x3, waiting for transfers between devices: none -> 46 us  [partner_sum(): lax.ppermute(send, AXIS_NAME, [(i, i ^ 1) for i in range(n_dev)])]
    add x0 -> x3, other arithmetic: none -> 29 us  [partner_sum(): keep + lax.ppermute(send, AXIS_NAME, [(i, i ^ 1) for i in range(n_dev)])]
    unnamed x71 -> x70, local copies, waits for them, and re-layouts: 35.1 us -> 33.1 us
  transfers between devices with their start and end apart: 10 -> 13, of which waited for: 5 -> 7; matrix products, arithmetic and copies ran while one was open for 16% -> 11% of each run, Pallas kernels for 31% -> 17%
where the time goes in v2:
time: 1560 us; the launch traced here: 1550 us
  waiting for transfers between devices  718 us (46%)
  Pallas kernels  454 us (29%)
  matrix products  164 us (11%)
  local copies, waits for them, and re-layouts  80.6 us (5%)
  other arithmetic  76.4 us (5%)
  blocking collectives  38 us (2%)
  between operations  16.5 us (1%)
    reduce_scatter x3, waiting for transfers between devices, scatter_rows_by_chip(): lax.psum_scatter(value, AXIS_NAME, scatter_dimension=0, tiled=True, axis_...  525 us
    reduce_scatter x2, waiting for transfers between devices, scatter_rows(): return lax.psum_scatter(grad, AXIS_NAME, scatter_dimension=0, tiled=True)  145 us
    pallas_call x1, Pallas kernels, table_scatter(): pl.pallas_call(functools.partial(scatter_body, group, slots, out_rows), g...  98.7 us
    dot_general x4, matrix products, dot_tn(): lax.dot_general(a, b, (((0,), (0,)), ((), ())), preferred_element_type=F32)  87.1 us
    pallas_call x1, Pallas kernels, attn_bwd(): pl.pallas_call(functools.partial(attn_bwd_body, kv_heads, rep, n_lead), g...  82.2 us
    pallas_call x1, Pallas kernels, table_gather(): pl.pallas_call(functools.partial(gather_body, n_tab, starts, tab_rows, to...  69.4 us
    pallas_call x2, Pallas kernels, norm_grad(): pl.pallas_call(functools.partial(norm_grad_body, as_rows, sub), grid=(tok...  68.4 us
    pallas_call x2, Pallas kernels, attn_fwd(): pl.pallas_call(functools.partial(attn_fwd_body, kv_heads, rep, into is no...  64.1 us
  transfers between devices with their start and end apart: 13, of which 7 were waited for; matrix products, arithmetic and copies ran while one was open for 11% of the time, Pallas kernels for 17%

profile of v2, /device:TPU:0, one launch (start us, length us, event | category | flops | bytes accessed | tf_op | source)
XLA Modules:
  0.0 1548.4 jit_solution(17778598491526085033)
XLA Ops:
  8.1 1.1 fusion.24
  10.2 0.8 pad_maximum_fusion.9
  11.8 14.3 all_gather.18
  27.1 69.4 %table_gather.1 = (bf16[5120,8,128]{2,1,0:T(8,128)(2,1)}, bf16[5120,8,128]{2,1,0:T(8,128)(2,1)}, bf16[3072,8,128]{2,1,0:T(8,128)(2,1)}, bf16[3072,8,128]{2,1,0:T(8,128)(2,1)}) custom-call(s32[16384]{0:T(1024)} %pad_add_fusion.idx_ref, bf16[19008,1024]{1,0:T(8,128)(2,1)} %tab_ref.1), custom_call_target="tpu_custom_call" | custom-call | flops 70000001024 | bytes 72482816 | tf_op jit(solution)/shard_map/table_gather/pallas_call | solution.py:87
  96.5 10.4 collective-permute-done.1
  106.8 7.2 add.89
  114.1 1.0 copy-done.18
  115.2 1.0 pad_maximum_fusion.5
  116.5 16.2 %collective-permute-done = bf16[5120,8,128]{2,1,0:T(8,128)(2,1)S(1)} collective-permute-done((bf16[5120,8,128]{2,1,0:T(8,128)(2,1)}, bf16[5120,8,128]{2,1,0:T(8,128)(2,1)S(1)}, u32[]{:S(2)}, u32[]{:S(2)}) %collective-permute-start) | collective-permute-done | bytes 10485792 | tf_op jit(solution)/shard_map/ppermute | solution.py:484
  132.7 10.9 add.88
  143.7 1.1 copy-done.16
  145.7 1.5 copy.53
  147.2 2.1 reshape.128
  150.0 3.7 fusion.15
  155.1 4.7 fusion.22
  159.8 46.9 %reduce-scatter.8.cloned.1.call-done = bf16[768,8,128]{2,1,0:T(8,128)(2,1)} async-done(((bf16[3072,8,128]{2,1,0:T(8,128)(2,1)}), bf16[768,8,128]{2,1,0:T(8,128)(2,1)}) %reduce-scatter.8.cloned.1.call-update) | async-done | bytes 1572880 | tf_op jit(solution)/shard_map/reduce_scatter | solution.py:490
  206.7 2.9 multiply_reduce_fusion.1
  209.6 3.0 copy.78
  212.6 14.0 convolution_convert_fusion.2.refs_0_.tail_ref
  226.6 145.9 %reduce-scatter.6.cloned.1.call-done = bf16[1280,8,128]{2,1,0:T(8,128)(2,1)} async-done(((bf16[5120,8,128]{2,1,0:T(8,128)(2,1)}), bf16[1280,8,128]{2,1,0:T(8,128)(2,1)}) %reduce-scatter.6.cloned.1.call-update) | async-done | bytes 2621456 | tf_op jit(solution)/shard_map/reduce_scatter | solution.py:490
  372.4 10.9 multiply_reduce_fusion
  383.3 17.9 %convolution_convert_fusion.refs_0_.lead_ref = bf16[1280,4096]{1,0:T(8,128)(2,1)} fusion(bf16[1024,4096]{1,0:T(8,128)(2,1)} %all-gather.8.cloned.1.call-done.w_ref, f32[1024]{0:T(1024)S(1)} %bitcast.97, f32[1280]{0:T(1024)S(1)} %add_rsqrt_fusion.2, bf16[160,8,8,128]{3,2,1,0:T(8,128)(2,1)} %bitcast.77), kind=kOutput, calls=%fused_computation.1 | convolution fusion | flops 10747904000 | bytes 21505024 | tf_op jit(solution)/shard_map/dot_general | solution.py:29
  401.2 4.0 copy-done.6
  405.2 39.8 %attn_fwd.2.refs_5_ = bf16[2048,2048]{1,0:T(8,128)(2,1)S(1)} custom-call(bf16[1280,4096]{1,0:T(8,128)(2,1)S(1)} %copy-done.6, f32[2048,128]{1,0:T(8,128)S(1)} %get-tuple-element.100.refs_1_.cos_ref, f32[2048,128]{1,0:T(8,128)S(1)} %get-tuple-element.101.refs_2_.sin_ref, f32[1,128]{1,0:T(1,128)S(1)} %get-tuple-element.103.refs_3_.qn_ref, ...), custom_call_target="tpu_custom_call" | custom-call | flops 24999999488 | bytes 15728640 | tf_op jit(solution)/shard_map/attn_fwd/pallas_call | solution.py:328
  445.7 24.3 %attn_fwd.3 = bf16[2048,2048]{1,0:T(8,128)(2,1)S(1)} custom-call(bf16[768,4096]{1,0:T(8,128)(2,1)S(1)} %bitcast.73, f32[2048,128]{1,0:T(8,128)S(1)} %get-tuple-element.100.refs_1_.cos_ref, f32[2048,128]{1,0:T(8,128)S(1)} %get-tuple-element.101.refs_2_.sin_ref, f32[1,128]{1,0:T(1,128)S(1)} %get-tuple-element.103.refs_3_.qn_ref, ...), custom_call_target="tpu_custom_call", output_to_operand_aliasing={{}: (5, {})} | custom-call | flops 24999999488 | bytes 9437184 | tf_op jit(solution)/shard_map/attn_fwd/pallas_call | solution.py:328
  470.2 2.3 copy-done.11
  472.7 2.1 copy-done.13
  474.8 12.2 fusion.3
  487.1 2.0 copy-done.12
  489.1 2.5 fusion.5.x_ref
  491.6 2.2 copy-done.1
  493.8 36.8 %swiglu_fwd.1 = (f32[2048,6144]{1,0:T(8,128)}, bf16[2048,3072]{1,0:T(8,128)(2,1)}) custom-call(bf16[2048,1024]{1,0:T(8,128)(2,1)S(1)} %copy-done.1, bf16[1024,6144]{1,0:T(8,128)(2,1)} %all-gather.10.cloned.1.call-done.w_ref), custom_call_target="tpu_custom_call" | custom-call | flops 25769803776 | bytes 62914560 | tf_op jit(solution)/shard_map/swiglu_fwd/pallas_call | solution.py:379
  530.6 18.0 %fusion.27 = f32[3072,1024]{1,0:T(8,128)} fusion(bf16[2048,3072]{1,0:T(8,128)(2,1)} %get-tuple-element.60, bf16[2048,1024]{1,0:T(8,128)(2,1)S(1)} %bitcast.70), kind=kOutput, calls=%fused_computation.78 | convolution fusion | flops 12884901888 | bytes 29360128 | tf_op jit(solution)/shard_map/dot_general | solution.py:25
  548.6 2.8 copy-done
  551.4 2.2 copy-done.4
  553.6 34.0 %swiglu_bwd.1.g_ref = bf16[2048,6144]{1,0:T(8,128)(2,1)} custom-call(bf16[2048,1024]{1,0:T(8,128)(2,1)S(1)} %bitcast.71, bf16[3072,1024]{1,0:T(8,128)(2,1)S(1)} %copy-done, f32[2048,6144]{1,0:T(8,128)} %get-tuple-element.54.gu_ref), custom_call_target="tpu_custom_call" | custom-call | flops 12884901888 | bytes 75497472 | tf_op jit(solution)/shard_map/swiglu_bwd/pallas_call | solution.py:405
  587.6 31.6 %fusion.28 = f32[1024,6144]{1,0:T(8,128)} fusion(bf16[2048,1024]{1,0:T(8,128)(2,1)S(1)} %copy-done.2, bf16[2048,6144]{1,0:T(8,128)(2,1)} %swiglu_bwd.1.g_ref), kind=kOutput, calls=%fused_computation.79 | convolution fusion | flops 25769803776 | bytes 54525952 | tf_op jit(solution)/shard_map/dot_general | solution.py:25
  619.2 38.6 %shard_map.246 = (f32[2048,1024]{1,0:T(8,128)}, bf16[2048,1024]{1,0:T(8,128)(2,1)}, f32[8,1024]{1,0:T(8,128)}) custom-call(bf16[2048,6144]{1,0:T(8,128)(2,1)} %swiglu_bwd.1.g_ref, bf16[1024,6144]{1,0:T(8,128)(2,1)} %all-gather.10.cloned.1.call-done.w_ref, bf16[2048,1024]{1,0:T(8,128)(2,1)} %copy-done.12, bf16[2048,1024]{1,0:T(8,128)(2,1)} %bitcast.69, ...), custom_call_target="tpu_custom_call" | custom-call | flops 25769803776 | bytes 62914560 | tf_op jit(solution)/shard_map/pallas_call | solution.py:457
  657.9 13.9 convolution_convert_fusion.1.do_ref
  671.8 2.8 copy-done.7
  674.6 82.2 %attn_bwd.1 = (bf16[2048,4096]{1,0:T(8,128)(2,1)}, f32[8,128]{1,0:T(8,128)S(1)}, f32[8,128]{1,0:T(8,128)S(1)}) custom-call(bf16[1280,4096]{1,0:T(8,128)(2,1)} %convolution_convert_fusion.refs_0_.lead_ref, bf16[768,4096]{1,0:T(8,128)(2,1)S(1)} %copy-done.7, bf16[2048,2048]{1,0:T(8,128)(2,1)} %convolution_convert_fusion.1.do_ref, ...), custom_call_target="tpu_custom_call" | custom-call | flops 99999997952 | bytes 41943040 | tf_op jit(solution)/shard_map/attn_bwd/pallas_call | solution.py:349
  756.7 29.8 %shard_map.247 = (f32[16384,128]{1,0:T(8,128)}, f32[8,1024]{1,0:T(8,128)}) custom-call(bf16[2048,4096]{1,0:T(8,128)(2,1)} %get-tuple-element.69.g_ref, bf16[1024,4096]{1,0:T(8,128)(2,1)} %all-gather.8.cloned.1.call-done.w_ref, bf16[2048,1024]{1,0:T(8,128)(2,1)} %copy-done.8, f32[2048,1024]{1,0:T(8,128)} %get-tuple-element.58.res_ref, f32[1,1024]{1,0:T(1,128)} %copy-done.23), custom_call_target="tpu_custom_call" | custom-call | flops 17179869184 | bytes 50331648 | tf_op jit(solution)/shard_map/pallas_call | solution.py:457
  786.5 14.8 fusion.29
  801.4 7.2 fusion.21
  808.6 0.9 fusion
  809.5 22.6 %fusion.7 = f32[1024,4096]{1,0:T(8,128)S(1)} fusion(bf16[2048,4096]{1,0:T(8,128)(2,1)} %get-tuple-element.69.g_ref, bf16[2048,1024]{1,0:T(8,128)(2,1)} %copy-done.8, f32[1024]{0:T(1024)S(1)} %bitcast.98, f32[2048]{0:T(1024)S(1)} %add_rsqrt_fusion), kind=kOutput, calls=%fused_computation.22 | convolution fusion | flops 17188257792 | bytes 37761024 | tf_op jit(solution)/shard_map/dot_general | solution.py:25
  832.2 13.5 pad_maximum_fusion
  845.6 10.6 dynamic-slice_bitcast_fusion
  856.2 19.4 %collective-permute-done.2 = f32[4,128,6144]{2,1,0:T(8,128)S(1)} collective-permute-done((f32[4,128,6144]{2,1,0:T(8,128)}, f32[4,128,6144]{2,1,0:T(8,128)S(1)}, u32[]{:S(2)}, u32[]{:S(2)}) %collective-permute-start.2) | collective-permute-done | bytes 12582944 | tf_op jit(solution)/shard_map/ppermute | solution.py:484
  875.6 10.9 bitcast_add_fusion
  888.7 6.4 sort.15
  895.2 0.8 convert_reduce_fusion.bst_ref
  897.6 23.7 %psum.7 = f32[2304]{0:T(1024)S(1)} all-reduce(f32[2304]{0:T(1024)S(1)} %pad_maximum_fusion.10), channel_id=1, replica_groups=mesh['fsdp'=8] {'fsdp'}, use_global_device_ids=true, to_apply=%region_7.8 | all-reduce | flops 2304 | bytes 18432 | tf_op jit(solution)/shard_map/psum | solution.py:607
  921.8 19.2 %fusion.6 = bf16[2048,1024]{1,0:T(8,128)(2,1)} fusion(bf16[2048,1024]{1,0:T(8,128)(2,1)} %copy-done.12, bf16[2048,3072]{1,0:T(8,128)(2,1)} %get-tuple-element.60, bf16[3072,1024]{1,0:T(8,128)(2,1)} %all-gather.12.cloned.1.call-done.w_ref), kind=kOutput, calls=%fused_computation.15 | convolution fusion | flops 12891193344 | bytes 27262976 | tf_op jit(solution)/shard_map/dot_general | solution.py:29
  941.0 331.7 %reduce-scatter.10.cloned.1.call-done = f32[128,6144]{1,0:T(8,128)} async-done(((f32[512,6144]{1,0:T(8,128)}), f32[128,6144]{1,0:T(8,128)}) %reduce-scatter.10.cloned.1.call-update) | async-done | bytes 3145744 | tf_op jit(solution)/shard_map/reduce_scatter | solution.py:490
  1272.7 2.3 split.20
  1275.0 2.7 fusion.23
  1277.7 1.0 pad_maximum_fusion.8
  1278.7 145.4 %reduce-scatter.12.cloned.1.call-done = f32[128,6144]{1,0:T(8,128)} async-done(((f32[1024,6144]{1,0:T(8,128)}), f32[128,6144]{1,0:T(8,128)}) %reduce-scatter.12.cloned.1.call-update) | async-done | bytes 3145744 | tf_op jit(solution)/shard_map/reduce_scatter | solution.py:479
  1424.1 4.1 reshape.134
  1428.2 8.9 slice_reduce_fusion
  1437.2 2.4 copy.66
  1439.5 2.4 copy.65
  1441.9 98.7 %table_scatter.1 = f32[19008,1024]{1,0:T(8,128)} custom-call(s32[16384]{0:T(1024)S(1)} %get-tuple-element.61.perm_ref, s32[16384]{0:T(1024)S(1)} %get-tuple-element.62.sid_ref, s32[67]{0:T(128)S(1)} %convert_reduce_fusion.bst_ref, f32[16384,8,128]{2,1,0:T(8,128)} %all-gather.14.cloned.1.call-done.rows_ref), custom_call_target="tpu_custom_call" | custom-call | flops 70000001024 | bytes 144965632 | tf_op jit(solution)/shard_map/table_scatter/pallas_call | solution.py:162
  (120 shorter events, 11.5 us)
Async XLA Ops:
  8.0 146.3 %all-gather.6.cloned.1.call-start = ((), (), s32[]{:S(2)}) async-start(), calls=%async_computation.7 | async-start | bytes 5013504 | tf_op jit(solution)/shard_map/all_gather | solution.py:475
  11.0 195.7 %reduce-scatter.8.cloned.1.call-start = ((), (), s32[]{:S(2)}) async-start(), calls=%async_computation.6 | async-start | bytes 7864320 | tf_op jit(solution)/shard_map/reduce_scatter | solution.py:490
  26.2 70.3 %copy-start.14 = (s32[16384]{0:T(1024)}, s32[16384]{0:T(1024)S(1)}, u32[]{:S(2)}) copy-start(s32[16384]{0:T(1024)S(1)} %and_select_fusion) | copy-start | bytes 196612
  96.5 10.4 collective-permute-start.1
  114.0 1.0 copy-start.18
  114.0 1.1 copy-start.19
  114.0 1.2 copy-start.20
  114.0 98.5 %all-gather.8.cloned.1.call-start = ((), (), s32[]{:S(2)}) async-start(), calls=%async_computation.8 | async-start | bytes 9437184 | tf_op jit(solution)/shard_map/all_gather | solution.py:475
  116.3 256.2 %reduce-scatter.6.cloned.1.call-start = ((), (), s32[]{:S(2)}) async-start(), calls=%async_computation.5 | async-start | bytes 13107200 | tf_op jit(solution)/shard_map/reduce_scatter | solution.py:490
  116.3 16.4 %collective-permute-start = (bf16[5120,8,128]{2,1,0:T(8,128)(2,1)}, bf16[5120,8,128]{2,1,0:T(8,128)(2,1)S(1)}, u32[]{:S(2)}, u32[]{:S(2)}) collective-permute-start(bf16[5120,8,128]{2,1,0:T(8,128)(2,1)} %get-tuple-element.44), channel_id=1, source_target_pairs={{0,1},{1,0},{2,3},{3,2},{4,5},{5,4},{6,7},{7,6}} | collective-permute-start | bytes 31457288 | tf_op jit(solution)/shard_map/ppermute | solution.py:484
  143.6 1.1 copy-start.16
  143.6 1.5 copy-start.17
  143.6 348.0 %all-gather.10.cloned.1.call-start = ((), (), s32[]{:S(2)}) async-start(), calls=%async_computation.9 | async-start | bytes 14155776 | tf_op jit(solution)/shard_map/all_gather | solution.py:475
  145.7 4.2 copy-start.22
  145.7 4.3 copy-start.25
  145.7 4.3 copy-start.26
  149.3 399.3 %all-gather.12.cloned.1.call-start = ((), (), s32[]{:S(2)}) async-start(), calls=%async_computation.10 | async-start | bytes 7077888 | tf_op jit(solution)/shard_map/all_gather | solution.py:475
  149.8 1122.9 %reduce-scatter.10.cloned.1.call-start = ((), (), s32[]{:S(2)}) async-start(), calls=%async_computation.12 | async-start | bytes 15728640 | tf_op jit(solution)/shard_map/reduce_scatter | solution.py:490
  155.1 228.3 %copy-start.23 = (f32[1,1024]{1,0:T(1,128)}, f32[1,1024]{1,0:T(1,128)S(1)}, u32[]{:S(2)}) copy-start(f32[1,1024]{1,0:T(1,128)S(1)} %get-tuple-element.95.gain_ref) | copy-start | bytes 12292
  155.1 332.0 %copy-start.21 = (f32[1,1024]{1,0:T(1,128)}, f32[1,1024]{1,0:T(1,128)S(1)}, u32[]{:S(2)}) copy-start(f32[1,1024]{1,0:T(1,128)S(1)} %get-tuple-element.94.gain_ref) | copy-start | bytes 12292
  383.3 62.3 %slice-start = ((s8[6291456]{0:T(1024)(128)(4,1)}), s8[4194304]{0:T(1024)(128)(4,1)S(1)}, s32[]{:S(2)}) async-start(s8[6291456]{0:T(1024)(128)(4,1)} %bitcast.72), calls=%async_computation.15 | async-start | bytes 8388608
  401.2 4.0 copy-start.6
  405.2 39.8 %copy-start.10 = (bf16[1280,8,128]{2,1,0:T(8,128)(2,1)S(1)}, bf16[1280,8,128]{2,1,0:T(8,128)(2,1)}, u32[]{:S(2)}) copy-start(bf16[1280,8,128]{2,1,0:T(8,128)(2,1)} %reduce-scatter.6.cloned.1.call-done) | copy-start | bytes 7864324
  405.2 40.5 %slice-start.1 = ((s8[6291456]{0:T(1024)(128)(4,1)}), s8[2097152]{0:T(1024)(128)(4,1)S(1)}, s32[]{:S(2)}) async-start(s8[6291456]{0:T(1024)(128)(4,1)} %bitcast.72), calls=%async_computation.16 | async-start | bytes 4194304
  470.0 17.1 %copy-start.5 = (bf16[2048,2048]{1,0:T(8,128)(2,1)}, bf16[2048,2048]{1,0:T(8,128)(2,1)S(1)}, u32[]{:S(2)}) copy-start(bf16[2048,2048]{1,0:T(8,128)(2,1)S(1)} %attn_fwd.3) | copy-start | bytes 25165828
  470.0 2.6 copy-start.11
  470.0 4.8 copy-start.13
  472.7 14.4 copy-start.8
  487.0 2.0 copy-start.12
  491.6 2.2 copy-start.1
  493.8 36.8 %copy-start.3 = (bf16[8,256,1024]{2,1,0:T(8,128)(2,1)S(1)}, bf16[8,256,1024]{2,1,0:T(8,128)(2,1)}, u32[]{:S(2)}) copy-start(bf16[8,256,1024]{2,1,0:T(8,128)(2,1)} %param.29) | copy-start | bytes 12582916
  548.6 2.8 copy-start
  551.4 2.2 copy-start.4
  553.6 34.1 %copy-start.2 = (bf16[2048,1024]{1,0:T(8,128)(2,1)S(1)}, bf16[2048,1024]{1,0:T(8,128)(2,1)}, u32[]{:S(2)}) copy-start(bf16[2048,1024]{1,0:T(8,128)(2,1)} %fusion.5.x_ref) | copy-start | bytes 12582916
  671.8 2.8 copy-start.7
  801.4 7.2 copy-start.9
  801.4 8.1 copy-start.24
  856.2 19.4 %collective-permute-start.2 = (f32[4,128,6144]{2,1,0:T(8,128)}, f32[4,128,6144]{2,1,0:T(8,128)S(1)}, u32[]{:S(2)}, u32[]{:S(2)}) collective-permute-start(f32[4,128,6144]{2,1,0:T(8,128)} %dynamic-slice_bitcast_fusion), channel_id=1, source_target_pairs={{0,1},{1,0},{2,3},{3,2},{4,5},{5,4},{6,7},{7,6}} | collective-permute-start | bytes 37748744 | tf_op jit(solution)/shard_map/ppermute | solution.py:484
  886.5 537.6 %reduce-scatter.12.cloned.1.call-start = ((), (), s32[]{:S(2)}) async-start(), calls=%async_computation.13 | async-start | bytes 28311552 | tf_op jit(solution)/shard_map/reduce_scatter | solution.py:479
  887.3 554.7 %all-gather.14.cloned.1.call-start = ((), (), s32[]{:S(2)}) async-start(), calls=%async_computation.11 | async-start | bytes 75497472 | tf_op jit(solution)/shard_map/all_gather | solution.py:475
  887.9 0.8 copy-start.15
  887.9 652.8 %reduce-scatter.14.cloned.1.call-start = ((), (), s32[]{:S(2)}) async-start(), calls=%async_computation.14 | async-start | bytes 14155776 | tf_op jit(solution)/shard_map/reduce_scatter | solution.py:479
Sparse Core Ops, SparseCore 0:
  11.2 36.0 all-gather.5
  117.2 72.7 all-gather.7
  192.5 79.2 all-gather.9
  273.5 61.7 all-gather.11
  889.6 326.5 all-gather.13
Sparse Core Ops, SparseCore 1:
  114.1 92.5 reduce-scatter.7
  210.2 162.2 reduce-scatter.5
  886.6 386.0 reduce-scatter.9
  1276.3 147.8 reduce-scatter.11
  1428.1 83.7 reduce-scatter.13

commit v3 on v2

--- a/solution.py
+++ b/solution.py
@@ -48,13 +48,19 @@
     @pl.when(step < n_tab)
     def _():
         for lane in range(SUBL):
-            stage[pl.ds(lane, tab_rows, stride=SUBL), :] = tab_ref[:, lane * LANES:(lane + 1) * LANES].astype(F32)
-        rows = stage[...].reshape(tab_rows, SUBL, LANES)
-        store[pl.ds(step * tab_rows, tab_rows)] = rows.astype(BF16)
+            stage[pl.ds(lane, tab_rows, stride=SUBL + 1), :] = tab_ref[:, lane * LANES:(lane + 1) * LANES].astype(F32)
+
+        def put(it, carry):
+            for u in range(32):
+                row = it * 32 + u
+                store[step * tab_rows + row] = stage[pl.ds(row * (SUBL + 1), SUBL), :].astype(BF16)
+            return carry
+
+        lax.fori_loop(0, tab_rows // 32, put, 0)
 
     def copy_rows(out_ref):
         base = (step - n_tab) * tok_rows
-        unroll = 16
+        unroll = 32
 
         def loop(it, carry):
             first = it * unroll
@@ -72,7 +78,7 @@
 
 def table_gather(table, idx, counts):
     rows, width = table.shape
-    tab_rows = block_of(rows, 640, 16)
+    tab_rows = block_of(rows, 640, 32)
     n_tab = rows // tab_rows
     tok_rows = 512
     starts = [sum(counts[:k]) // tok_rows for k in range(len(counts) + 1)]
@@ -82,7 +88,7 @@
         grid=(n_tab + starts[-1],),
         in_specs=[pl.BlockSpec((tab_rows, width), lambda s, ids: (jnp.minimum(s, n_tab - 1), 0))],
         out_specs=[out_spec(lo, hi) for lo, hi in zip(starts, starts[1:])],
-        scratch_shapes=[pltpu.VMEM((rows + 8, SUBL, LANES), BF16), pltpu.VMEM((tab_rows * SUBL, LANES), F32)],
+        scratch_shapes=[pltpu.VMEM((rows + 8, SUBL, LANES), BF16), pltpu.VMEM((tab_rows * (SUBL + 1), LANES), F32)],
     )
     return pl.pallas_call(
         functools.partial(gather_body, n_tab, starts, tab_rows, tok_rows),
@@ -213,7 +219,7 @@
     return pl.ds(pl.multiple_of(start, LANES), width)
 
 
-KV_UNROLL = 2
+KV_UNROLL = 4
 
 
 def attn_fwd_body(kv_heads, rep, aliased, *refs):
@@ -533,7 +539,7 @@
         out_half = w_out.shape[0] // 2
         gain_cols = jnp.pad(jnp.stack([attn_norm, mlp_norm], axis=1), ((0, 0), (0, LANES - 2)))
         w_o = gather_rows(jnp.concatenate([w_out[:out_half], w_out[out_half:], gain_cols], axis=1))
-        n_lead = 5 * n_seq // 8
+        n_lead = n_seq // 2
         lead_tok = n_lead * seq
         core = lax.axis_index(AXIS_NAME) & 1
         n_chip = n_dev // 2

time: 1560 us -> 1540 us (0.987)
  waiting for transfers between devices: 718 us -> 746 us
  Pallas kernels: 454 us -> 427 us
    reduce_scatter x3, waiting for transfers between devices: 525 us -> 552 us  [scatter_rows_by_chip(): lax.psum_scatter(value, AXIS_NAME, scatter_dimension=0, tiled=True, axis_...]
    unnamed x70 -> x78, local copies, waits for them, and re-layouts: 33.1 us -> 28 us
  transfers between devices with their start and end apart: 13 -> 13, of which waited for: 7 -> 7; matrix products, arithmetic and copies ran while one was open for 11% -> 10% of each run, Pallas kernels for 17% -> 12%
where the time goes in v3:
time: 1540 us; the launch traced here: 1530 us
  waiting for transfers between devices  746 us (48%)
  Pallas kernels  427 us (28%)
  matrix products  158 us (10%)
  local copies, waits for them, and re-layouts  74.5 us (5%)
  other arithmetic  69 us (4%)
  blocking collectives  37.7 us (2%)
  between operations  16.6 us (1%)
    reduce_scatter x3, waiting for transfers between devices, scatter_rows_by_chip(): lax.psum_scatter(value, AXIS_NAME, scatter_dimension=0, tiled=True, axis_...  552 us
    reduce_scatter x2, waiting for transfers between devices, scatter_rows(): return lax.psum_scatter(grad, AXIS_NAME, scatter_dimension=0, tiled=True)  145 us
    pallas_call x1, Pallas kernels, table_scatter(): pl.pallas_call(functools.partial(scatter_body, group, slots, out_rows), g...  98.7 us
    dot_general x4, matrix products, dot_tn(): lax.dot_general(a, b, (((0,), (0,)), ((), ())), preferred_element_type=F32)  87 us
    pallas_call x1, Pallas kernels, attn_bwd(): pl.pallas_call(functools.partial(attn_bwd_body, kv_heads, rep, n_lead), g...  75.8 us
    pallas_call x2, Pallas kernels, norm_grad(): pl.pallas_call(functools.partial(norm_grad_body, as_rows, sub), grid=(tok...  68.4 us
    pallas_call x1, Pallas kernels, table_gather(): pl.pallas_call(functools.partial(gather_body, n_tab, starts, tab_rows, to...  61.2 us
    dot_general x4, matrix products, dot_nn(): return jnp.dot(a, b, preferred_element_type=F32)  56.8 us
  transfers between devices with their start and end apart: 13, of which 7 were waited for; matrix products, arithmetic and copies ran while one was open for 10% of the time, Pallas kernels for 12%

profile of v3, /device:TPU:0, one launch (start us, length us, event | category | flops | bytes accessed | tf_op | source)
XLA Modules:
  0.0 1530.1 jit_solution(14499151639525717957)
XLA Ops:
  8.1 0.7 copy.61
  8.8 13.8 all_gather.18
  23.5 61.2 %table_gather.1 = (bf16[4096,8,128]{2,1,0:T(8,128)(2,1)}, bf16[4096,8,128]{2,1,0:T(8,128)(2,1)}, bf16[4096,8,128]{2,1,0:T(8,128)(2,1)}, bf16[4096,8,128]{2,1,0:T(8,128)(2,1)}) custom-call(s32[16384]{0:T(1024)} %pad_add_fusion.idx_ref, bf16[19008,1024]{1,0:T(8,128)(2,1)} %tab_ref.1), custom_call_target="tpu_custom_call" | custom-call | flops 70000001024 | bytes 72482816 | tf_op jit(solution)/shard_map/table_gather/pallas_call | solution.py:93
  85.2 0.8 pad_maximum_fusion.9
  86.1 12.1 collective-permute-done
  98.3 10.0 add.82
  108.5 14.8 collective-permute-done.1
  123.3 8.2 add.83
  131.5 0.9 copy-done.19
  132.6 1.0 pad_maximum_fusion.5
  134.7 1.5 copy.53
  136.2 2.1 reshape.128
  139.2 3.7 fusion.15
  143.6 0.7 convert_bitcast_fusion
  144.3 4.6 fusion.22
  149.0 87.1 %reduce-scatter.6.cloned.1.call-done = bf16[1024,8,128]{2,1,0:T(8,128)(2,1)} async-done(((bf16[4096,8,128]{2,1,0:T(8,128)(2,1)}), bf16[1024,8,128]{2,1,0:T(8,128)(2,1)}) %reduce-scatter.6.cloned.1.call-update) | async-done | bytes 2097168 | tf_op jit(solution)/shard_map/reduce_scatter | solution.py:496
  236.1 3.7 multiply_reduce_fusion
  239.8 133.6 %reduce-scatter.8.cloned.1.call-done = bf16[1024,8,128]{2,1,0:T(8,128)(2,1)} async-done(((bf16[4096,8,128]{2,1,0:T(8,128)(2,1)}), bf16[1024,8,128]{2,1,0:T(8,128)(2,1)}) %reduce-scatter.8.cloned.1.call-update) | async-done | bytes 2097168 | tf_op jit(solution)/shard_map/reduce_scatter | solution.py:496
  373.4 3.5 multiply_reduce_fusion.1
  377.0 13.5 convolution_convert_fusion.1.refs_0_.lead_ref
  390.5 25.8 %attn_fwd.2.refs_5_ = bf16[2048,2048]{1,0:T(8,128)(2,1)S(1)} custom-call(bf16[1024,4096]{1,0:T(8,128)(2,1)S(1)} %convolution_convert_fusion.1.refs_0_.lead_ref, f32[2048,128]{1,0:T(8,128)S(1)} %get-tuple-element.104.refs_1_.cos_ref, f32[2048,128]{1,0:T(8,128)S(1)} %get-tuple-element.105.refs_2_.sin_ref, f32[1,128]{1,0:T(1,128)S(1)} %get-tuple-element.107.refs_3_.qn_ref, ...), custom_call_target="tpu_custom_call" | custom-call | flops 24999999488 | bytes 12582912 | tf_op jit(solution)/shard_map/attn_fwd/pallas_call | solution.py:334
  416.3 11.4 convolution_convert_fusion.2.refs_0_.tail_ref
  429.1 26.0 %attn_fwd.3 = bf16[2048,2048]{1,0:T(8,128)(2,1)S(1)} custom-call(bf16[1024,4096]{1,0:T(8,128)(2,1)S(1)} %convolution_convert_fusion.2.refs_0_.tail_ref, f32[2048,128]{1,0:T(8,128)S(1)} %get-tuple-element.104.refs_1_.cos_ref, f32[2048,128]{1,0:T(8,128)S(1)} %get-tuple-element.105.refs_2_.sin_ref, ...), custom_call_target="tpu_custom_call", output_to_operand_aliasing={{}: (5, {})} | custom-call | flops 24999999488 | bytes 12582912 | tf_op jit(solution)/shard_map/attn_fwd/pallas_call | solution.py:334
  455.0 3.2 copy-done.6
  458.6 2.9 copy-done.5
  461.6 12.7 fusion.3
  474.4 2.0 copy-done.13
  476.3 2.5 fusion.5.x_ref
  478.8 2.2 copy-done.1
  481.0 36.8 %swiglu_fwd.1 = (f32[2048,6144]{1,0:T(8,128)}, bf16[2048,3072]{1,0:T(8,128)(2,1)}) custom-call(bf16[2048,1024]{1,0:T(8,128)(2,1)S(1)} %copy-done.1, bf16[1024,6144]{1,0:T(8,128)(2,1)} %all-gather.10.cloned.1.call-done.w_ref), custom_call_target="tpu_custom_call" | custom-call | flops 25769803776 | bytes 62914560 | tf_op jit(solution)/shard_map/swiglu_fwd/pallas_call | solution.py:385
  517.8 17.9 %fusion.27 = f32[3072,1024]{1,0:T(8,128)} fusion(bf16[2048,3072]{1,0:T(8,128)(2,1)} %get-tuple-element.60, bf16[2048,1024]{1,0:T(8,128)(2,1)S(1)} %bitcast.90), kind=kOutput, calls=%fused_computation.86 | convolution fusion | flops 12884901888 | bytes 29360128 | tf_op jit(solution)/shard_map/dot_general | solution.py:25
  535.7 2.8 copy-done
  538.5 2.2 copy-done.4
  540.6 34.2 %swiglu_bwd.1.g_ref = bf16[2048,6144]{1,0:T(8,128)(2,1)} custom-call(bf16[2048,1024]{1,0:T(8,128)(2,1)S(1)} %bitcast.91, bf16[3072,1024]{1,0:T(8,128)(2,1)S(1)} %copy-done, f32[2048,6144]{1,0:T(8,128)} %get-tuple-element.54.gu_ref), custom_call_target="tpu_custom_call" | custom-call | flops 12884901888 | bytes 75497472 | tf_op jit(solution)/shard_map/swiglu_bwd/pallas_call | solution.py:411
  574.9 31.7 %fusion.28 = f32[1024,6144]{1,0:T(8,128)} fusion(bf16[2048,1024]{1,0:T(8,128)(2,1)S(1)} %copy-done.2, bf16[2048,6144]{1,0:T(8,128)(2,1)} %swiglu_bwd.1.g_ref), kind=kOutput, calls=%fused_computation.87 | convolution fusion | flops 25769803776 | bytes 54525952 | tf_op jit(solution)/shard_map/dot_general | solution.py:25
  606.5 38.4 %shard_map.246 = (f32[2048,1024]{1,0:T(8,128)}, bf16[2048,1024]{1,0:T(8,128)(2,1)}, f32[8,1024]{1,0:T(8,128)}) custom-call(bf16[2048,6144]{1,0:T(8,128)(2,1)} %swiglu_bwd.1.g_ref, bf16[1024,6144]{1,0:T(8,128)(2,1)} %all-gather.10.cloned.1.call-done.w_ref, bf16[2048,1024]{1,0:T(8,128)(2,1)} %copy-done.13, bf16[2048,1024]{1,0:T(8,128)(2,1)} %bitcast.89, ...), custom_call_target="tpu_custom_call" | custom-call | flops 25769803776 | bytes 62914560 | tf_op jit(solution)/shard_map/pallas_call | solution.py:463
  645.0 14.3 convolution_convert_fusion.do_ref
  659.2 3.4 copy-done.8
  662.6 75.8 %attn_bwd.1 = (bf16[2048,4096]{1,0:T(8,128)(2,1)}, f32[8,128]{1,0:T(8,128)S(1)}, f32[8,128]{1,0:T(8,128)S(1)}) custom-call(bf16[1024,4096]{1,0:T(8,128)(2,1)S(1)} %copy-done.8, bf16[1024,4096]{1,0:T(8,128)(2,1)} %copy-done.6, bf16[2048,2048]{1,0:T(8,128)(2,1)} %convolution_convert_fusion.do_ref, f32[2048,128]{1,0:T(8,128)S(1)} %get-tuple-element.104.refs_1_.cos_ref, ...), custom_call_target="tpu_custom_call" | custom-call | flops 99999997952 | bytes 41943040 | tf_op jit(solution)/shard_map/attn_bwd/pallas_call | solution.py:355
  738.4 29.9 %shard_map.247 = (f32[16384,128]{1,0:T(8,128)}, f32[8,1024]{1,0:T(8,128)}) custom-call(bf16[2048,4096]{1,0:T(8,128)(2,1)} %get-tuple-element.69.g_ref, bf16[1024,4096]{1,0:T(8,128)(2,1)} %all-gather.8.cloned.1.call-done.w_ref, bf16[2048,1024]{1,0:T(8,128)(2,1)} %copy-done.9, f32[2048,1024]{1,0:T(8,128)} %get-tuple-element.58.res_ref, f32[1,1024]{1,0:T(1,128)} %copy-done.24), custom_call_target="tpu_custom_call" | custom-call | flops 17179869184 | bytes 50331648 | tf_op jit(solution)/shard_map/pallas_call | solution.py:463
  768.4 14.6 fusion.29
  783.0 7.3 fusion.21
  790.3 0.9 fusion
  791.2 22.8 %fusion.7 = f32[1024,4096]{1,0:T(8,128)S(1)} fusion(bf16[2048,4096]{1,0:T(8,128)(2,1)} %get-tuple-element.69.g_ref, bf16[2048,1024]{1,0:T(8,128)(2,1)} %copy-done.9, f32[1024]{0:T(1024)S(1)} %bitcast.120, f32[2048]{0:T(1024)S(1)} %add_rsqrt_fusion), kind=kOutput, calls=%fused_computation.20 | convolution fusion | flops 17188257792 | bytes 37761024 | tf_op jit(solution)/shard_map/dot_general | solution.py:25
  814.1 13.3 pad_maximum_fusion
  827.3 10.6 dynamic-slice_bitcast_fusion
  837.9 19.4 %collective-permute-done.2 = f32[4,128,6144]{2,1,0:T(8,128)S(1)} collective-permute-done((f32[4,128,6144]{2,1,0:T(8,128)}, f32[4,128,6144]{2,1,0:T(8,128)S(1)}, u32[]{:S(2)}, u32[]{:S(2)}) %collective-permute-start.2) | collective-permute-done | bytes 12582944 | tf_op jit(solution)/shard_map/ppermute | solution.py:490
  857.3 10.9 bitcast_add_fusion
  870.4 6.4 sort.15
  876.9 0.8 convert_reduce_fusion.bst_ref
  877.7 0.8 slice.75
  878.5 0.8 slice.74
  879.3 23.8 %psum.7 = f32[2304]{0:T(1024)S(1)} all-reduce(f32[2304]{0:T(1024)S(1)} %pad_maximum_fusion.10), channel_id=1, replica_groups=mesh['fsdp'=8] {'fsdp'}, use_global_device_ids=true, to_apply=%region_7.8 | all-reduce | flops 2304 | bytes 18432 | tf_op jit(solution)/shard_map/psum | solution.py:613
  903.7 19.2 %fusion.6 = bf16[2048,1024]{1,0:T(8,128)(2,1)} fusion(bf16[2048,1024]{1,0:T(8,128)(2,1)} %copy-done.13, bf16[2048,3072]{1,0:T(8,128)(2,1)} %get-tuple-element.60, bf16[3072,1024]{1,0:T(8,128)(2,1)} %all-gather.12.cloned.1.call-done.w_ref), kind=kOutput, calls=%fused_computation.14 | convolution fusion | flops 12891193344 | bytes 27262976 | tf_op jit(solution)/shard_map/dot_general | solution.py:29
  922.9 331.4 %reduce-scatter.10.cloned.1.call-done = f32[128,6144]{1,0:T(8,128)} async-done(((f32[512,6144]{1,0:T(8,128)}), f32[128,6144]{1,0:T(8,128)}) %reduce-scatter.10.cloned.1.call-update) | async-done | bytes 3145744 | tf_op jit(solution)/shard_map/reduce_scatter | solution.py:496
  1254.3 2.3 split.20
  1256.6 2.7 fusion.23
  1259.3 1.0 pad_maximum_fusion.8
  1260.3 145.4 %reduce-scatter.12.cloned.1.call-done = f32[128,6144]{1,0:T(8,128)} async-done(((f32[1024,6144]{1,0:T(8,128)}), f32[128,6144]{1,0:T(8,128)}) %reduce-scatter.12.cloned.1.call-update) | async-done | bytes 3145744 | tf_op jit(solution)/shard_map/reduce_scatter | solution.py:485
  1405.8 4.1 reshape.134
  1409.9 8.9 slice_reduce_fusion
  1418.8 2.4 copy.70
  1421.2 2.4 copy.69
  1423.6 98.7 %table_scatter.1 = f32[19008,1024]{1,0:T(8,128)} custom-call(s32[16384]{0:T(1024)S(1)} %get-tuple-element.61.perm_ref, s32[16384]{0:T(1024)S(1)} %get-tuple-element.62.sid_ref, s32[67]{0:T(128)S(1)} %convert_reduce_fusion.bst_ref, f32[16384,8,128]{2,1,0:T(8,128)} %all-gather.14.cloned.1.call-done.rows_ref), custom_call_target="tpu_custom_call" | custom-call | flops 70000001024 | bytes 144965632 | tf_op jit(solution)/shard_map/table_scatter/pallas_call | solution.py:168
  (119 shorter events, 8.7 us)
Async XLA Ops:
  8.0 135.6 %all-gather.6.cloned.1.call-start = ((), (), s32[]{:S(2)}) async-start(), calls=%async_computation.7 | async-start | bytes 5013504 | tf_op jit(solution)/shard_map/all_gather | solution.py:481
  22.6 62.1 %copy-start.14 = (s32[16384]{0:T(1024)}, s32[16384]{0:T(1024)S(1)}, u32[]{:S(2)}) copy-start(s32[16384]{0:T(1024)S(1)} %and_select_fusion) | copy-start | bytes 196612
  23.5 61.3 %copy-start.18 = (bf16[256,1024]{1,0:T(8,128)(2,1)S(1)}, bf16[256,1024]{1,0:T(8,128)(2,1)}, u32[]{:S(2)}) copy-start(bf16[256,1024]{1,0:T(8,128)(2,1)} %param.24) | copy-start | bytes 1572868
  23.5 61.7 %copy-start.26 = (bf16[128]{0:T(256)(128)(2,1)S(1)}, bf16[128]{0:T(256)(128)(2,1)}, u32[]{:S(2)}) copy-start(bf16[128]{0:T(256)(128)(2,1)} %param.25) | copy-start | bytes 772
  23.5 61.7 %copy-start.27 = (bf16[128]{0:T(256)(128)(2,1)S(1)}, bf16[128]{0:T(256)(128)(2,1)}, u32[]{:S(2)}) copy-start(bf16[128]{0:T(256)(128)(2,1)} %param.18) | copy-start | bytes 772
  84.8 13.5 collective-permute-start
  86.1 150.0 %reduce-scatter.6.cloned.1.call-start = ((), (), s32[]{:S(2)}) async-start(), calls=%async_computation.5 | async-start | bytes 10485760 | tf_op jit(solution)/shard_map/reduce_scatter | solution.py:496
  108.2 265.2 %reduce-scatter.8.cloned.1.call-start = ((), (), s32[]{:S(2)}) async-start(), calls=%async_computation.6 | async-start | bytes 10485760 | tf_op jit(solution)/shard_map/reduce_scatter | solution.py:496
  108.3 15.0 collective-permute-start.1
  131.4 1.0 copy-start.19
  131.4 1.1 copy-start.20
  131.4 1.2 copy-start.21
  131.4 2.3 copy-start.16
  131.5 2.7 copy-start.17
  131.5 245.5 %all-gather.8.cloned.1.call-start = ((), (), s32[]{:S(2)}) async-start(), calls=%async_computation.8 | async-start | bytes 9437184 | tf_op jit(solution)/shard_map/all_gather | solution.py:481
  133.7 345.1 %all-gather.10.cloned.1.call-start = ((), (), s32[]{:S(2)}) async-start(), calls=%async_computation.9 | async-start | bytes 14155776 | tf_op jit(solution)/shard_map/all_gather | solution.py:481
  134.7 4.5 copy-start.23
  134.7 4.5 copy-start.28
  134.7 4.5 copy-start.29
  138.3 397.4 %all-gather.12.cloned.1.call-start = ((), (), s32[]{:S(2)}) async-start(), calls=%async_computation.10 | async-start | bytes 7077888 | tf_op jit(solution)/shard_map/all_gather | solution.py:481
  138.9 1115.5 %reduce-scatter.10.cloned.1.call-start = ((), (), s32[]{:S(2)}) async-start(), calls=%async_computation.12 | async-start | bytes 15728640 | tf_op jit(solution)/shard_map/reduce_scatter | solution.py:496
  144.3 272.0 %copy-start.24 = (f32[1,1024]{1,0:T(1,128)}, f32[1,1024]{1,0:T(1,128)S(1)}, u32[]{:S(2)}) copy-start(f32[1,1024]{1,0:T(1,128)S(1)} %get-tuple-element.99.gain_ref) | copy-start | bytes 12292
  144.3 330.0 %copy-start.22 = (f32[1,1024]{1,0:T(1,128)}, f32[1,1024]{1,0:T(1,128)S(1)}, u32[]{:S(2)}) copy-start(f32[1,1024]{1,0:T(1,128)S(1)} %get-tuple-element.98.gain_ref) | copy-start | bytes 12292
  390.5 25.8 %copy-start.7 = (bf16[1024,4096]{1,0:T(8,128)(2,1)}, bf16[1024,4096]{1,0:T(8,128)(2,1)S(1)}, u32[]{:S(2)}) copy-start(bf16[1024,4096]{1,0:T(8,128)(2,1)S(1)} %convolution_convert_fusion.1.refs_0_.lead_ref) | copy-start | bytes 25165828
  390.5 25.8 %copy-start.12 = (bf16[1024,8,128]{2,1,0:T(8,128)(2,1)S(1)}, bf16[1024,8,128]{2,1,0:T(8,128)(2,1)}, u32[]{:S(2)}) copy-start(bf16[1024,8,128]{2,1,0:T(8,128)(2,1)} %reduce-scatter.8.cloned.1.call-done) | copy-start | bytes 6291460
  416.3 11.5 copy-start.11
  455.0 3.2 copy-start.6
  458.3 3.3 copy-start.5
  458.6 15.7 %copy-start.9 = (bf16[2048,1024]{1,0:T(8,128)(2,1)}, bf16[2048,1024]{1,0:T(8,128)(2,1)S(1)}, u32[]{:S(2)}) copy-start(bf16[2048,1024]{1,0:T(8,128)(2,1)S(1)} %constant_dynamic-update-slice_fusion.x_ref) | copy-start | bytes 12582916
  474.3 2.0 copy-start.13
  478.8 2.2 copy-start.1
  481.0 36.8 %copy-start.3 = (bf16[8,256,1024]{2,1,0:T(8,128)(2,1)S(1)}, bf16[8,256,1024]{2,1,0:T(8,128)(2,1)}, u32[]{:S(2)}) copy-start(bf16[8,256,1024]{2,1,0:T(8,128)(2,1)} %param.29) | copy-start | bytes 12582916
  535.7 2.8 copy-start
  538.5 2.2 copy-start.4
  540.6 34.2 %copy-start.2 = (bf16[2048,1024]{1,0:T(8,128)(2,1)S(1)}, bf16[2048,1024]{1,0:T(8,128)(2,1)}, u32[]{:S(2)}) copy-start(bf16[2048,1024]{1,0:T(8,128)(2,1)} %fusion.5.x_ref) | copy-start | bytes 12582916
  659.2 3.4 copy-start.8
  783.0 7.3 copy-start.10
  790.3 0.9 copy-start.25
  837.9 19.4 %collective-permute-start.2 = (f32[4,128,6144]{2,1,0:T(8,128)}, f32[4,128,6144]{2,1,0:T(8,128)S(1)}, u32[]{:S(2)}, u32[]{:S(2)}) collective-permute-start(f32[4,128,6144]{2,1,0:T(8,128)} %dynamic-slice_bitcast_fusion), channel_id=1, source_target_pairs={{0,1},{1,0},{2,3},{3,2},{4,5},{5,4},{6,7},{7,6}} | collective-permute-start | bytes 37748744 | tf_op jit(solution)/shard_map/ppermute | solution.py:490
  868.2 537.5 %reduce-scatter.12.cloned.1.call-start = ((), (), s32[]{:S(2)}) async-start(), calls=%async_computation.13 | async-start | bytes 28311552 | tf_op jit(solution)/shard_map/reduce_scatter | solution.py:485
  869.0 554.6 %all-gather.14.cloned.1.call-start = ((), (), s32[]{:S(2)}) async-start(), calls=%async_computation.11 | async-start | bytes 75497472 | tf_op jit(solution)/shard_map/all_gather | solution.py:481
  869.6 0.8 copy-start.15
  869.6 652.8 %reduce-scatter.14.cloned.1.call-start = ((), (), s32[]{:S(2)}) async-start(), calls=%async_computation.14 | async-start | bytes 14155776 | tf_op jit(solution)/shard_map/reduce_scatter | solution.py:485
Sparse Core Ops, SparseCore 0:
  86.2 34.5 all-gather.5
  134.7 62.9 all-gather.7
  200.1 75.7 all-gather.9
  277.5 54.0 all-gather.11
  871.3 326.5 all-gather.13
Sparse Core Ops, SparseCore 1:
  108.3 127.7 reduce-scatter.5
  239.6 133.8 reduce-scatter.7
  868.3 386.0 reduce-scatter.9
  1257.9 147.8 reduce-scatter.11
  1409.8 83.7 reduce-scatter.13
